TPU v7x, 32 devices: a whole 2x2x4 slice. The times are simulated.
32 devices in a mesh: row: 4 (over y, core), col: 8 (over z, x).
Axes of the slice: x: 2, y: 2, z: 4, core: 2. Of those that a mesh axis runs over, the one named last changes fastest.
Arguments:
- l_saved: bfloat16 [16, 4, 256, 8, 256], P(None, 'row', None, 'col'), as said below
- l_grad: bfloat16 [16, 4, 256, 8, 256], P(None, 'row', None, 'col'), as said below
Outputs:
- grad_out: float32 [16, 4, 256, 8, 256], P(None, 'row', None, 'col')
Inputs may be any that keep to these rules, and one draw needn't show every extreme that they name: Read as one matrix of 16384 rows, l_saved is lower triangular with its diagonal between 1 and 2. Read as one matrix, l_grad is zero above the diagonal.
All inputs are finite; a program needn't handle non-finite values.
Results may differ from a plain program's by a relative error of at most 0.0003.
Values may be sent and summed in bfloat16 or wider, within the bound.
A program may use at most 64 MiB of HBM per device.

v0:
```python
import functools

import jax
import jax.numpy as jnp
from jax import lax
from jax.experimental import pallas as pl
from jax.experimental.pallas import tpu as pltpu
from jax.sharding import PartitionSpec as P

F32 = jnp.float32
BF16 = jnp.bfloat16
HIGH3 = lax.Precision.HIGH


def dot3(a, b, ca=1, cb=0):
    return lax.dot_general(
        a, b, (((ca,), (cb,)), ((), ())), precision=HIGH3, preferred_element_type=F32
    )


def bdot(a, b):
    return lax.dot_general(
        a, b, (((2,), (1,)), ((0,), (0,))), precision=HIGH3, preferred_element_type=F32
    )


def inverse_pair(tiles):
    tile = tiles.shape[-1]
    rows = lax.broadcasted_iota(jnp.int32, (tile, tile), 0)
    cols = lax.broadcasted_iota(jnp.int32, (tile, tile), 1)
    eye = (rows == cols).astype(F32)
    recip = 1.0 / jnp.sum(tiles * eye, axis=2)
    inv = eye * recip[:, None, :]
    size = 1
    while size < tile:
        off = (rows // size % 2 == 1) & (cols // size == rows // size - 1)
        part = jnp.where(off, tiles, 0.0)
        if size == 1:
            inv = inv - recip[:, :, None] * part * recip[:, None, :]
        else:
            inv = inv - bdot(inv, bdot(part, inv))
        size *= 2
    return inv


def spread_kernel(n_col, in_ref, out_ref, send_sem, recv_sem):
    n = in_ref.shape[0]
    ring = n_col // 2
    col = lax.axis_index("col")
    q, p = col // 2, col % 2
    up = lax.rem(q + 1, ring) * 2 + p
    down = lax.rem(q + ring - 1, ring) * 2 + p
    twin = 2 * q + 1 - p

    barrier = pltpu.get_barrier_semaphore()
    for peer in (up, down, twin):
        pl.semaphore_signal(barrier, inc=1, device_id={"col": peer}, device_id_type=pl.DeviceIdType.MESH)
    pl.semaphore_wait(barrier, 3)

    k_of = (lax.rem(q + 1, ring), ring - 1 - q)
    nexts = (up, down)
    backs = (down, up)
    streams = [(s, d) for s in (0, 1) for d in (0, 1)]

    def copy(src, s, t, slot, dev):
        return pltpu.make_async_remote_copy(
            src_ref=src.at[t],
            dst_ref=out_ref.at[s, t],
            send_sem=send_sem.at[s, t, slot],
            recv_sem=recv_sem.at[s, t],
            device_id={"col": dev},
            device_id_type=pl.DeviceIdType.MESH,
        )

    def roles(s, d, idx):
        k = k_of[d]
        main = p == s
        once = idx % 3 == 0
        source = main & (k == 0)
        fwd = (main | once) & (k < ring - 1)
        cross = main & jnp.where(once, k == 0, k > 0)
        back = jnp.logical_not(once) & jnp.logical_not(main) & (k == 1)
        return source, fwd, cross, back

    half = (n + 1) // 2

    def step(j, _):
        for s, d in streams:
            lag = k_of[d] + jnp.where(p == s, 0, 1)
            idx = j - lag
            t = 2 * idx + d
            live = (idx >= 0) & (t < n)
            source, fwd, cross, back = roles(s, d, idx)
            moves = fwd | cross | back

            @pl.when(live & source)
            def _():
                @pl.when(fwd)
                def _():
                    copy(in_ref, s, t, 0, nexts[d]).start()

                @pl.when(cross)
                def _():
                    copy(in_ref, s, t, 1, twin).start()

            @pl.when(live & moves & jnp.logical_not(source))
            def _():
                copy(out_ref.at[s], s, t, 0, twin).wait_recv()

                @pl.when(fwd)
                def _():
                    copy(out_ref.at[s], s, t, 0, nexts[d]).start()

                @pl.when(cross)
                def _():
                    copy(out_ref.at[s], s, t, 1, twin).start()

                @pl.when(back)
                def _():
                    copy(out_ref.at[s], s, t, 0, backs[d]).start()

        return 0

    lax.fori_loop(0, half + ring + 1, step, 0)

    for s in (0, 1):

        @pl.when(col == n_col - 2 + s)
        def _():
            def keep(t, _):
                out_ref[s, t] = in_ref[t]
                return 0

            lax.fori_loop(0, n, keep, 0)

    def finish(idx, _):
        for s, d in streams:
            t = 2 * idx + d
            live = t < n
            source, fwd, cross, back = roles(s, d, idx)
            moves = fwd | cross | back

            @pl.when(live & jnp.logical_not(moves) & jnp.logical_not(source))
            def _():
                copy(out_ref.at[s], s, t, 0, twin).wait_recv()

            @pl.when(live & (fwd | back))
            def _():
                copy(out_ref.at[s], s, t, 0, twin).wait_send()

            @pl.when(live & cross)
            def _():
                copy(out_ref.at[s], s, t, 1, twin).wait_send()

        return 0

    lax.fori_loop(0, half, finish, 0)


def spread(mine, n_col):
    n, tile = mine.shape[0], mine.shape[1]
    vmem = pl.BlockSpec(memory_space=pltpu.VMEM)
    return pl.pallas_call(
        functools.partial(spread_kernel, n_col),
        out_shape=jax.ShapeDtypeStruct((2, n, tile, tile), mine.dtype),
        in_specs=[vmem],
        out_specs=vmem,
        scratch_shapes=[pltpu.SemaphoreType.DMA((2, n, 2)), pltpu.SemaphoreType.DMA((2, n))],
        compiler_params=pltpu.CompilerParams(collective_id=0, has_side_effects=True),
        name="spread",
    )(mine)


def per_device(l_saved, l_grad):
    rows_here, tile = l_saved.shape[0], l_saved.shape[2]
    n_row = lax.axis_size("row")
    n_col = lax.axis_size("col")
    factor = l_saved.reshape(rows_here, tile, tile)
    grad = l_grad.reshape(rows_here, tile, tile)
    my_row = lax.axis_index("row")
    my_col = lax.axis_index("col")
    assert n_col % n_row == 0
    first = n_col // n_row
    loc = first - 1
    lo, hi = n_col - 2, n_col - 1

    l_rows = lax.all_gather(factor[loc], "row")[n_row - 2 :]
    l_dk = l_rows.reshape(2 * tile, tile)
    both = spread(jnp.concatenate([l_rows, grad[first:]], 0), n_col)
    l_dd = jnp.concatenate([both[i, :2].reshape(2 * tile, tile) for i in (0, 1)], 1).astype(F32)
    g_lo = both[0, 2:].reshape(-1, tile)
    g_hi = both[1, 2:].reshape(-1, tile)

    l66, l76, l77 = l_dd[:tile, :tile], l_dd[tile:, :tile], l_dd[tile:, tile:]
    inv = inverse_pair(jnp.stack([l66, l77]))
    w76 = -dot3(inv[1], dot3(l76, inv[0]))
    w = jnp.concatenate(
        [
            jnp.concatenate([inv[0], jnp.zeros_like(w76)], 1),
            jnp.concatenate([w76, inv[1]], 1),
        ],
        0,
    )

    below_l = factor[first:].reshape(-1, tile)
    h = jnp.concatenate(
        [
            lax.dot_general(g, below_l, (((0,), (0,)), ((), ())), preferred_element_type=F32)
            for g in (g_lo, g_hi)
        ],
        0,
    )
    t = dot3(w, lax.psum(h, "row"), 0, 0)

    fresh = grad[loc].astype(F32)
    g_dk = lax.all_gather(grad[loc], "row")[n_row - 2 :].reshape(2 * tile, tile).astype(F32)
    q_mine = g_dk - t
    z2 = jnp.zeros_like(q_mine)
    q = lax.psum(
        jnp.concatenate([jnp.where(my_col == lo, q_mine, z2), jnp.where(my_col == hi, q_mine, z2)], 1),
        "col",
    )
    eye2 = jnp.eye(2 * tile, dtype=F32)
    q = jnp.tril(q)
    m = dot3(l_dd, q, 0, 0)
    phi = jnp.tril(m) - 0.5 * m * eye2
    half = dot3(dot3(w, phi, 0, 0), w)
    s = half + half.T
    out_dd = jnp.tril(s) - 0.5 * s * eye2

    right = my_col >= lo
    w_mine = jnp.where(my_col == lo, w[:, :tile], w[:, tile:])
    x = jnp.where(right, -w_mine, dot3(w, l_dk.astype(F32)))
    x_hi = lax.reduce_precision(x, 8, 7)
    x_lo = (x - x_hi).astype(BF16)
    x_hi = x_hi.astype(BF16)
    prod = sum(
        jnp.dot(g, part[i * tile : (i + 1) * tile], preferred_element_type=F32)
        for part in (x_lo, x_hi)
        for i, g in enumerate((g_lo, g_hi))
    )
    base = jnp.where(right, jnp.zeros((), BF16), grad[first:]).astype(F32)
    low = base - prod.reshape(-1, tile, tile)

    at_lo = my_row == n_row - 2
    s_row = jnp.where(at_lo, s[:tile], s[tile:])
    t_row = jnp.where(at_lo, t[:tile], t[tile:])
    own = fresh - (t_row + dot3(s_row, l_dk.astype(F32)))
    d_row = jnp.where(at_lo, out_dd[:tile], out_dd[tile:])
    d_own = jnp.where(my_col == lo, d_row[:, :tile], d_row[:, tile:])
    in_panel = my_row >= n_row - 2
    zt = jnp.zeros_like(fresh)
    own = jnp.where(
        in_panel, jnp.where(right, d_own, own), jnp.where(right, zt, fresh)
    )
    upper = jnp.where(right, jnp.zeros((), BF16), grad[:loc]).astype(F32)
    out = jnp.concatenate([upper, own[None], low], 0)
    return out.reshape(l_grad.shape)


def solution(mesh):
    spec = P(None, "row", None, "col", None)
    return jax.shard_map(
        per_device, mesh=mesh, in_specs=(spec, spec), out_specs=spec, check_vma=False
    )
```

profile of v0, /device:TPU:5, one launch (start us, length us, event | category | flops | bytes accessed | tf_op | source)
XLA Modules:
  0.0 243.1 jit_solution(17539181726368961872)
XLA Ops:
  6.5 3.0 %slice.128 = bf16[14,1,256,1,256]{4,2,3,1,0:T(8,128)(2,1)} slice(bf16[16,1,256,1,256]{4,2,3,1,0:T(8,128)(2,1)} %param.2), slice={[2:16], [0:1], [0:256], [0:1], [0:256]} | slice | bytes 3670016 | tf_op jit(solution)/shard_map/slice | solution.py:205
  9.7 0.7 slice-done
  10.5 7.3 %all-gather = bf16[4,1,256,1,256]{4,2,3,1,0:T(8,128)(2,1)S(1)} all-gather(bf16[1,1,256,1,256]{4,2,3,1,0:T(8,128)(2,1)S(1)} %slice-done), channel_id=2, replica_groups=mesh['row'=4,'col'=8] {'row'}, dimensions={0}, use_global_device_ids=true | all-gather | bytes 655360 | tf_op jit(solution)/shard_map/all_gather | solution.py:187
  17.8 1.5 pad_maximum_fusion.in_ref
  19.3 79.7 %spread.1 = bf16[2,16,256,256]{3,2,1,0:T(8,128)(2,1)} custom-call(bf16[16,256,256]{2,1,0:T(8,128)(2,1)} %pad_maximum_fusion.in_ref), custom_call_target="tpu_custom_call" | custom-call | tf_op jit(solution)/shard_map/spread/pallas_call | solution.py:163
  99.0 2.5 %fusion.116 = (bf16[1,14,256,256]{3,2,1,0:T(8,128)(2,1)S(1)}, bf16[1,14,256,256]{3,2,1,0:T(8,128)(2,1)S(1)}) fusion(bf16[2,16,256,256]{3,2,1,0:T(8,128)(2,1)} %spread.1), kind=kLoop, calls=%fused_computation.236 | loop fusion | bytes 7340032 | tf_op jit(solution)/shard_map/slice | solution.py:192
  101.6 0.7 fusion.119
  102.8 0.7 fusion.120
  103.5 0.8 pad_maximum_fusion.4
  104.4 1.1 fusion.117
  106.8 0.5 fusion.29
  113.8 1.9 fusion.98
  115.8 1.4 convolution_negate_fusion
  117.2 1.7 bitcast_convert_fusion
  118.9 10.2 %all-gather.1 = bf16[4,1,256,1,256]{4,2,3,1,0:T(8,128)(2,1)S(1)} all-gather(bf16[1,1,256,1,256]{4,2,3,1,0:T(8,128)(2,1)S(1)} %get-tuple-element.12), channel_id=3, replica_groups=mesh['row'=4,'col'=8] {'row'}, dimensions={0}, use_global_device_ids=true | all-gather | bytes 655360 | tf_op jit(solution)/shard_map/all_gather | solution.py:216
  129.2 1.2 reduce-precision_convert_fusion
  130.4 0.6 fusion.96
  131.0 0.9 copy-done.1
  131.9 2.5 %convolution_add_fusion.2 = f32[3584,256]{1,0:T(8,128)} fusion(f32[3584,256]{1,0:T(8,128)S(1)} %fusion.96, bf16[3584,256]{1,0:T(8,128)(2,1)S(1)} %bitcast.83, bf16[512,256]{1,0:T(8,128)(2,1)S(1)} %get-tuple-element.18), kind=kOutput, calls=%fused_computation.2 | convolution fusion | flops 470679552 | bytes 9306112 | tf_op jit(solution)/shard_map/dot_general | solution.py:238
  134.4 2.7 %all-reduce.4.cloned.1.call-done = f32[512,256]{1,0:T(8,128)} async-done(((f32[512,256]{1,0:T(8,128)}), f32[512,256]{1,0:T(8,128)}) %all-reduce.4.cloned.1.call-update) | async-done | bytes 524304 | tf_op jit(solution)/shard_map/psum | solution.py:213
  137.0 2.7 %fusion.34 = (f32[512,256]{1,0:T(8,128)S(1)}, f32[512,256]{1,0:T(8,128)S(1)}, f32[512,256]{1,0:T(8,128)}) fusion(bf16[2,1,256,1,256]{4,2,3,1,0:T(8,128)(2,1)S(1)} %slice-done.1, pred[]{:T(512)S(6)} %eq.82, pred[]{:T(512)S(6)} %eq.101, f32[512,256]{1,0:T(8,128)} %all-reduce.4.cloned.1.call-done, f32[256,256]{1,0:T(8,128)S(1)} %get-tuple-element.22, ...), kind=kOutput, calls=%fused_computation.114 | convolution fusion | flops 404226048 | bytes 3145730 | tf_op jit(solution)/shard_map/dot_general | solution.py:16
  139.7 1.1 pad_maximum_fusion.1
  140.9 4.5 %convolution_add_fusion.1 = f32[3584,256]{1,0:T(8,128)} fusion(f32[3584,256]{1,0:T(8,128)} %convolution_add_fusion.2, bf16[3584,256]{1,0:T(8,128)(2,1)S(1)} %bitcast.80, bf16[512,256]{1,0:T(8,128)(2,1)S(1)} %copy-done.17), kind=kOutput, calls=%fused_computation.1 | convolution fusion | flops 470679552 | bytes 9306112 | tf_op jit(solution)/shard_map/dot_general | solution.py:238
  145.4 3.4 %convolution_add_fusion = f32[3584,256]{1,0:T(8,128)S(1)} fusion(f32[3584,256]{1,0:T(8,128)} %convolution_add_fusion.1, bf16[3584,256]{1,0:T(8,128)(2,1)} %bitcast.82, bf16[512,256]{1,0:T(8,128)(2,1)} %get-tuple-element.17), kind=kOutput, calls=%fused_computation | convolution fusion | flops 470679552 | bytes 9306112 | tf_op jit(solution)/shard_map/dot_general | solution.py:238
  148.9 2.3 convert_subtract_fusion
  151.1 70.1 %all-reduce.6.cloned.1.call-done = f32[512,512]{1,0:T(8,128)} async-done(((f32[512,512]{1,0:T(8,128)}), f32[512,512]{1,0:T(8,128)}) %all-reduce.6.cloned.1.call-update) | async-done | bytes 1048592 | tf_op jit(solution)/shard_map/psum | solution.py:219
  221.2 2.0 fusion.9
  223.3 1.0 fusion.4
  224.4 1.0 fusion.114
  225.3 1.3 copy.15
  226.7 1.6 select_subtract_fusion
  229.9 6.3 %copy.18 = f32[16,1,256,1,256]{4,3,2,1,0:T(1,128)} copy(f32[16,1,256,1,256]{4,2,0,3,1:T(8,128)S(1)} %maximum_bitcast_fusion) | data formatting | bytes 8388608 | tf_op jit(solution)/shard_map/reshape | solution.py:258
  (96 shorter events, 10.2 us)
Async XLA Ops:
  6.5 3.0 %copy-start.3 = (bf16[16,1,256,1,256]{4,2,3,1,0:T(8,128)(2,1)S(1)}, bf16[16,1,256,1,256]{4,2,3,1,0:T(8,128)(2,1)}, u32[]{:S(2)}) copy-start(bf16[16,1,256,1,256]{4,2,3,1,0:T(8,128)(2,1)} %param.3) | copy-start | bytes 6291460
  6.5 130.5 %all-reduce.4.cloned.1.call-start = ((), (), s32[]{:S(2)}) async-start(), calls=%async_computation | async-start | bytes 1048576 | tf_op jit(solution)/shard_map/psum | solution.py:213
  9.6 0.9 slice-start
  17.8 111.4 %copy-start.18 = (bf16[2,1,256,1,256]{4,2,0,3,1:T(8,128)(2,1)}, bf16[2,1,256,1,256]{4,2,0,3,1:T(8,128)(2,1)S(1)}, u32[]{:S(2)}) copy-start(bf16[2,1,256,1,256]{4,2,0,3,1:T(8,128)(2,1)S(1)} %get-tuple-element.19) | copy-start | bytes 786436
  99.0 2.6 %copy-start.15 = (bf16[14,1,256,1,256]{4,2,3,1,0:T(8,128)(2,1)S(1)}, bf16[14,1,256,1,256]{4,2,3,1,0:T(8,128)(2,1)}, u32[]{:S(2)}) copy-start(bf16[14,1,256,1,256]{4,2,3,1,0:T(8,128)(2,1)} %slice.128) | copy-start | bytes 5505028
  101.5 1.3 copy-start
  104.3 116.9 %all-reduce.6.cloned.1.call-start = ((), (), s32[]{:S(2)}) async-start(), calls=%async_computation.1 | async-start | bytes 2097152 | tf_op jit(solution)/shard_map/psum | solution.py:219
  105.4 0.8 copy-start.11
  105.4 0.8 copy-start.13
  115.7 21.3 %copy-start.5 = (f32[256,256]{1,0:T(8,128)}, f32[256,256]{1,0:T(8,128)S(1)}, u32[]{:S(2)}) copy-start(f32[256,256]{1,0:T(8,128)S(1)} %get-tuple-element.21) | copy-start | bytes 786436
  115.7 21.3 %copy-start.8 = (f32[256,256]{1,0:T(8,128)}, f32[256,256]{1,0:T(8,128)S(1)}, u32[]{:S(2)}) copy-start(f32[256,256]{1,0:T(8,128)S(1)} %get-tuple-element.22) | copy-start | bytes 786436
  129.1 1.3 copy-start.16
  130.4 1.5 copy-start.1
  131.9 5.1 %slice-start.1 = ((bf16[4,1,256,1,256]{4,2,3,1,0:T(8,128)(2,1)}), bf16[2,1,256,1,256]{4,2,3,1,0:T(8,128)(2,1)S(1)}, s32[]{:S(2)}) async-start(bf16[4,1,256,1,256]{4,2,3,1,0:T(8,128)(2,1)} %copy-done.16), calls=%async_computation.3 | async-start | bytes 524288 | tf_op jit(solution)/shard_map/slice | solution.py:216
  139.7 1.2 copy-start.17
  145.4 3.4 %copy-start.4 = (bf16[16,1,256,1,256]{4,2,3,1,0:T(8,128)(2,1)S(1)}, bf16[16,1,256,1,256]{4,2,3,1,0:T(8,128)(2,1)}, u32[]{:S(2)}) copy-start(bf16[16,1,256,1,256]{4,2,3,1,0:T(8,128)(2,1)} %param.3) | copy-start | bytes 6291460
  148.8 72.4 %copy-start.12 = (bf16[1,2,256,256]{3,2,1,0:T(8,128)(2,1)S(1)}, bf16[1,2,256,256]{3,2,1,0:T(8,128)(2,1)}, u32[]{:S(2)}) copy-start(bf16[1,2,256,256]{3,2,1,0:T(8,128)(2,1)} %copy-done.11) | copy-start | bytes 786436
  148.8 72.4 %copy-start.14 = (bf16[1,2,256,256]{3,2,1,0:T(8,128)(2,1)S(1)}, bf16[1,2,256,256]{3,2,1,0:T(8,128)(2,1)}, u32[]{:S(2)}) copy-start(bf16[1,2,256,256]{3,2,1,0:T(8,128)(2,1)} %copy-done.13) | copy-start | bytes 786436
  151.1 72.1 %copy-start.6 = (f32[256,256]{1,0:T(8,128)S(1)}, f32[256,256]{1,0:T(8,128)}, u32[]{:S(2)}) copy-start(f32[256,256]{1,0:T(8,128)} %copy-done.5) | copy-start | bytes 786436
  151.1 72.1 %copy-start.9 = (f32[256,256]{1,0:T(8,128)S(1)}, f32[256,256]{1,0:T(8,128)}, u32[]{:S(2)}) copy-start(f32[256,256]{1,0:T(8,128)} %copy-done.8) | copy-start | bytes 786436
  223.3 1.1 copy-start.7
  223.3 1.1 copy-start.10
  226.6 1.8 copy-start.19
  226.6 1.8 copy-start.21
  226.6 2.6 %copy-start.2 = (f32[14,256,256]{2,1,0:T(8,128)S(1)}, f32[14,256,256]{2,1,0:T(8,128)}, u32[]{:S(2)}) copy-start(f32[14,256,256]{2,1,0:T(8,128)} %convert_subtract_fusion) | copy-start | bytes 11010052
  228.3 1.2 copy-start.20
Sparse Core Ops, SparseCore 0:
  104.4 32.5 all-reduce.3
  141.0 80.2 all-reduce.5
where the time goes:
time: 245 us; the launch traced here: 243 us
  Pallas kernels  79.7 us (33%)
  waiting for transfers between devices  72.8 us (30%)
  matrix products  29.6 us (12%)
  local copies, waits for them, and re-layouts  18.1 us (7%)
  blocking collectives  17.5 us (7%)
  between operations  14 us (6%)
  other arithmetic  11.4 us (5%)
    pallas_call x1, Pallas kernels, spread(): pl.pallas_call(functools.partial(spread_kernel, n_col), out_shape=jax.Sha...  79.7 us
    psum x1, waiting for transfers between devices, per_device(): lax.psum(jnp.concatenate([jnp.where(my_col == lo, q_mine, z2), jnp.where(...  70.1 us
    dot_general x8, matrix products, dot3(): lax.dot_general(a, b, (((ca,), (cb,)), ((), ())), precision=HIGH3, prefer...  11.4 us
    dot_general x4, matrix products, per_device(): jnp.dot(g, part[i * tile:(i + 1) * tile], preferred_element_type=F32)  11.1 us
    all_gather x1, blocking collectives, per_device(): lax.all_gather(grad[loc], 'row')[n_row - 2:].reshape(2 * tile, tile)  10.2 us
    all_gather x1, blocking collectives, per_device(): l_rows = lax.all_gather(factor[loc], 'row')[n_row - 2:]  7.26 us
    reshape x1, local copies, waits for them, and re-layouts, per_device(): return out.reshape(l_grad.shape)  6.33 us
    dot_general x14, matrix products, bdot(): lax.dot_general(a, b, (((2,), (1,)), ((0,), (0,))), precision=HIGH3, pref...  5.75 us
  transfers between devices with their start and end apart: 2, of which 2 were waited for; matrix products, arithmetic and copies ran while one was open for 12% of the time, Pallas kernels for 0%

commit v1 on v0

v1 whole, which is shorter than its diff:
```python
import functools

import jax
import jax.numpy as jnp
from jax import lax
from jax.experimental import pallas as pl
from jax.experimental.pallas import tpu as pltpu
from jax.sharding import PartitionSpec as P

F32 = jnp.float32
BF16 = jnp.bfloat16
HIGH3 = lax.Precision.HIGH
MESH = pl.DeviceIdType.MESH
CHUNKS = 8


def dot3(a, b, ca=1, cb=0):
    return lax.dot_general(
        a, b, (((ca,), (cb,)), ((), ())), precision=HIGH3, preferred_element_type=F32
    )


def outer(a, b):
    return lax.dot_general(a, b, (((0,), (0,)), ((), ())), preferred_element_type=F32)


def panel_kernel(
    n_row,
    n_col,
    l_ref,
    g_ref,
    gbuf,
    xh,
    xl,
    own,
    lk,
    lbuf,
    w,
    h,
    tout,
    tin,
    tslot,
    hin,
    hsum,
    hslot,
    htwin,
    hfull,
    gd,
    sbuf,
    gs,
    gr,
    ls,
    lr,
    ks,
    kr,
    ts,
    tr,
    hs,
    hr,
    ds,
    dr,
    ss,
    sr,
):
    tile = l_ref.shape[1]
    half = tile // 2
    n = gbuf.shape[1]
    first = l_ref.shape[0] - n
    loc = first - 1
    ring = n_col // 2
    cut = n // 2
    head = min(2, n)
    pairs = n_row // 2

    row = lax.axis_index("row")
    col = lax.axis_index("col")
    q, p = col // 2, col % 2
    y, c = row // 2, row % 2
    panel = q == ring - 1
    top = y == pairs - 1
    lower = jnp.maximum(col - 2, 0)
    twin = 2 * q + 1 - p
    mate = 2 * y + 1 - c
    root = n_row - 2 + c

    rows = lax.broadcasted_iota(jnp.int32, (tile, tile), 0)
    cols = lax.broadcasted_iota(jnp.int32, (tile, tile), 1)

    def rdma(src, dst, s_sem, r_sem, dev):
        return pltpu.make_async_remote_copy(
            src_ref=src, dst_ref=dst, send_sem=s_sem, recv_sem=r_sem, device_id=dev, device_id_type=MESH
        )

    barrier = pltpu.get_barrier_semaphore()

    def greet(dev):
        pl.semaphore_signal(barrier, inc=1, device_id=dev, device_id_type=MESH)

    greet({"col": twin})
    greet({"row": mate})

    @pl.when(q > 0)
    def _():
        greet({"col": col - 2})

    @pl.when(jnp.logical_not(panel))
    def _():
        greet({"col": col + 2})

    @pl.when(jnp.logical_not(top))
    def _():
        greet({"row": root})

    @pl.when(top)
    def _():
        for k in range(pairs - 1):
            greet({"row": 2 * k + c})

    @pl.when(top & panel)
    def _():
        greet({"row": mate, "col": twin})

    heard = (
        2
        + (q > 0).astype(jnp.int32)
        + jnp.logical_not(panel).astype(jnp.int32)
        + jnp.where(top, pairs - 1, 1)
        + (top & panel).astype(jnp.int32)
    )
    pl.semaphore_wait(barrier, heard)

    def g_down(t, src):
        return rdma(src, gbuf.at[p, t], gs.at[t, 0], gr.at[p, t], {"col": lower})

    def g_cross(t, src):
        return rdma(src, gbuf.at[p, t], gs.at[t, 1], gr.at[p, t], {"col": twin})

    def g_wait(s, t):
        rdma(gbuf.at[s, t], gbuf.at[s, t], gs.at[t, 0], gr.at[s, t], {"col": twin}).wait_recv()

    def f_cross(t):
        return rdma(l_ref.at[first + t], gbuf.at[0, t], gs.at[t, 1], gr.at[0, t], {"col": twin})

    def l_down(i, src):
        return rdma(src, lbuf.at[p, i], ls.at[i, 0], lr.at[p, i], {"col": lower})

    def l_cross(i, src):
        return rdma(src, lbuf.at[p, i], ls.at[i, 1], lr.at[p, i], {"col": twin})

    def l_wait(s, i):
        rdma(lbuf.at[s, i], lbuf.at[s, i], ls.at[i, 0], lr.at[s, i], {"col": twin}).wait_recv()

    def k_star(k):
        return rdma(l_ref.at[loc], lk.at[c], ks.at[k], kr.at[c], {"row": 2 * k + c})

    def k_mate(src):
        return rdma(src, lk.at[c], ks.at[pairs], kr.at[c], {"row": mate})

    def k_wait(i):
        rdma(lk.at[i], lk.at[i], ks.at[pairs], kr.at[i], {"row": mate}).wait_recv()

    def t_mate():
        return rdma(tout.at[1 - c], tin, ts.at[0], tr.at[pairs], {"row": mate})

    def t_root():
        return rdma(tout.at[c], tslot.at[y], ts.at[1], tr.at[y], {"row": root})

    def h_mate(k):
        return rdma(h.at[k, 1 - c], hin.at[k], hs.at[k, 0], hr.at[k, 0], {"row": mate})

    def h_root(k):
        return rdma(hsum.at[k], hslot.at[k, y], hs.at[k, 1], hr.at[k, 3 + y], {"row": root})

    def h_twin(k):
        return rdma(hsum.at[k], htwin.at[k], hs.at[k, 2], hr.at[k, 1], {"col": twin})

    def h_full(k):
        return rdma(hfull.at[k, c], hfull.at[k, c], hs.at[k, 3], hr.at[k, 2], {"row": mate})

    def d_mate(k):
        return rdma(g_ref.at[loc], gd.at[k], ds.at[0], dr.at[k], {"row": mate})

    def d_twin(k):
        return rdma(g_ref.at[loc], gd.at[k], ds.at[1], dr.at[k], {"col": twin})

    def d_diag(k):
        return rdma(g_ref.at[loc], gd.at[k], ds.at[2], dr.at[k], {"row": mate, "col": twin})

    def s_down(k):
        return rdma(sbuf.at[p, k], sbuf.at[p, k], ss.at[k, 0], sr.at[p, k], {"col": lower})

    def s_cross(k):
        return rdma(sbuf.at[p, k], sbuf.at[p, k], ss.at[k, 1], sr.at[p, k], {"col": twin})

    def loop(a, b, body):
        def step(i, carry):
            body(i)
            return carry

        lax.fori_loop(a, b, step, 0)

    def when_p0(cond, body):
        pl.when(cond)(body)

    @pl.when(top)
    def _():
        for k in range(pairs - 1):
            k_star(k).start()
        k_mate(l_ref.at[loc]).start()
        lk[c] = l_ref[loc]

    def gather_rows():
        @pl.when(jnp.logical_not(top))
        def _():
            k_wait(c)
            k_mate(lk.at[c]).start()

        k_wait(1 - c)

    def start_inverse():
        for k in range(2):
            d = lbuf[k, k].astype(F32)
            e = (rows == cols).astype(F32)
            on = d * e
            rc = 1.0 / jnp.sum(on, axis=1, keepdims=True)
            rr = 1.0 / jnp.sum(on, axis=0, keepdims=True)
            off = ((rows & 1) == 1) & (cols == rows - 1)
            w[k] = e * rr - rc * jnp.where(off, d, 0.0) * rr

    levels = []
    size = 2
    while size < tile:
        levels.append(size)
        size *= 2

    def inverse_level(size):
        sh = size.bit_length() - 1
        off = (((rows >> sh) & 1) == 1) & ((cols >> sh) == (rows >> sh) - 1)
        for k in range(2):
            part = jnp.where(off, lbuf[k, k].astype(F32), 0.0)
            cur = w[k]
            w[k] = cur - dot3(cur, dot3(part, cur))

    def finish_inverse():
        w[2] = -dot3(w[1], dot3(lbuf[0, 1].astype(F32), w[0]))

    def put_x(i, x):
        hi = x.astype(BF16)
        xh[i] = hi
        xl[i] = (x - hi.astype(F32)).astype(BF16)

    h[...] = jnp.zeros_like(h)

    def add_h(k, left, right):
        h[k] += outer(left, right).reshape(2, half, tile)

    @pl.when(jnp.logical_not(panel))
    def _():
        def relay(t):
            g_wait(p, t)

            @pl.when(q > 0)
            def _():
                g_down(t, gbuf.at[p, t]).start()

            g_cross(t, gbuf.at[p, t]).start()

        def relay_l(i):
            l_wait(p, i)

            @pl.when(q > 0)
            def _():
                l_down(i, lbuf.at[p, i]).start()

            l_cross(i, lbuf.at[p, i]).start()

        def use(t):
            g_wait(1 - p, t)
            right = l_ref[first + t]
            add_h(0, gbuf[0, t], right)
            add_h(1, gbuf[1, t], right)

        for t in range(head):
            relay(t)
        gather_rows()

        @pl.when(p == 0)
        def _():
            relay_l(0)

        relay_l(1)

        @pl.when(p == 0)
        def _():
            l_wait(1, 1)

        @pl.when(p == 1)
        def _():
            l_wait(0, 0)
            l_wait(0, 1)

        def solve_x():
            finish_inverse()
            k0, k1 = lk[0].astype(F32), lk[1].astype(F32)
            put_x(0, dot3(w[0], k0))
            put_x(1, dot3(w[2], k0) + dot3(w[1], k1))

        work = [start_inverse] + [functools.partial(inverse_level, s) for s in levels] + [solve_x]
        t = head
        for job in work:
            if t < n:
                relay(t)
                use(t - 2)
                t += 1
            job()
        done = t

        def both(i):
            relay(i)
            use(i - 2)

        if done < n:
            loop(done, n, both)
        loop(max(n - 2, 0), n, use)

        h0, h1 = h[0].reshape(tile, tile), h[1].reshape(tile, tile)
        tout[1] = dot3(w[1], h1, 0, 0)
        tout[0] = dot3(w[0], h0, 0, 0) + dot3(w[2], h1, 0, 0)
        t_mate().start()

        @pl.when(jnp.logical_not(top))
        def _():
            t_mate().wait_recv()
            tout[c] += tin[...]
            t_root().start()
            own[...] = g_ref[loc].astype(F32)

        @pl.when(top)
        def _():
            def s_wait(s, k):
                rdma(sbuf.at[s, k], sbuf.at[s, k], ss.at[k, 0], sr.at[s, k], {"col": twin}).wait_recv()

            def s_relay(k):
                s_wait(p, k)

                @pl.when(q > 0)
                def _():
                    s_down(k).start()

                s_cross(k).start()

            loop(0, CHUNKS, s_relay)
            t_mate().wait_recv()
            total = g_ref[loc].astype(F32) - (tout[c] + tin[...])
            for k in range(pairs - 1):
                rdma(tslot.at[k], tslot.at[k], ts.at[1], tr.at[k], {"row": mate}).wait_recv()
                total = total - tslot[k]
            own[...] = total
            loop(0, CHUNKS, lambda k: s_wait(1 - p, k))
            k0, k1 = lk[0].astype(F32), lk[1].astype(F32)
            s0, s1 = sbuf[0].reshape(tile, tile), sbuf[1].reshape(tile, tile)
            own[...] -= dot3(s0, k0) + dot3(s1, k1)

        def drain_g(t):
            @pl.when(q > 0)
            def _():
                g_down(t, gbuf.at[p, t]).wait_send()

            g_cross(t, gbuf.at[p, t]).wait_send()

        loop(0, n, drain_g)

        def drain_l(i):
            @pl.when(q > 0)
            def _():
                l_down(i, lbuf.at[p, i]).wait_send()

            l_cross(i, lbuf.at[p, i]).wait_send()

        @pl.when(p == 0)
        def _():
            drain_l(0)

        drain_l(1)
        t_mate().wait_send()

        @pl.when(jnp.logical_not(top))
        def _():
            t_root().wait_send()

        @pl.when(top)
        def _():
            def drain_s(k):
                @pl.when(q > 0)
                def _():
                    s_down(k).wait_send()

                s_cross(k).wait_send()

            loop(0, CHUNKS, drain_s)

    @pl.when(panel)
    def _():
        def send(t):
            if ring > 1:
                g_down(t, g_ref.at[first + t]).start()

        def cross_lo(t):
            f_cross(t).start()

        def cross_hi(t):
            g_cross(t, g_ref.at[first + t]).start()

        lead = min(2, cut)
        for t in range(head):
            send(t)

        @pl.when(p == 0)
        def _():
            for t in range(cut, min(cut + 2, n)):
                cross_lo(t)

        @pl.when(p == 1)
        def _():
            for t in range(lead):
                cross_hi(t)

        gather_rows()

        @pl.when(p == 0)
        def _():
            for i in range(2):
                if ring > 1:
                    l_down(i, lk.at[i]).start()
                l_cross(i, lk.at[i]).start()
                lbuf[0, i] = lk[i]
            loop(min(cut + 2, n), n, cross_lo)

            @pl.when(top & (c == 1))
            def _():
                d_mate(1).start()
                d_diag(1).start()
                gd[1] = g_ref[loc]

        @pl.when(p == 1)
        def _():
            if ring > 1:
                l_down(1, lk.at[1]).start()
            l_cross(1, lk.at[1]).start()
            lbuf[1, 1] = lk[1]
            loop(lead, cut, cross_hi)

            @pl.when(top & (c == 1))
            def _():
                d_mate(2).start()
                d_twin(2).start()
                d_diag(2).start()
                gd[2] = g_ref[loc]

        loop(head, n, send)

        loop(0, n, lambda t: add_h(0, g_ref[first + t], l_ref[first + t]))
        h_mate(0).start()

        @pl.when(p == 0)
        def _():
            l_wait(1, 1)

        @pl.when(p == 1)
        def _():
            l_wait(0, 0)
            l_wait(0, 1)

        def reduce_mate(k):
            h_mate(k).wait_recv()
            hsum[k] = h[k, c] + hin[k]

            @pl.when(jnp.logical_not(top))
            def _():
                h_root(k).start()

        def reduce_root(k):
            total = hsum[k]
            for i in range(pairs - 1):
                rdma(
                    hslot.at[k, i], hslot.at[k, i], hs.at[k, 1], hr.at[k, 3 + i], {"row": mate}
                ).wait_recv()
                total = total + hslot[k, i]
            hsum[k] = total
            h_twin(k).start()

        start_inverse()
        reduce_mate(0)
        for i, s in enumerate(levels):
            inverse_level(s)
            if i == len(levels) // 2:

                @pl.when(top)
                def _():
                    reduce_root(0)

        finish_inverse()

        def keep(t):
            gbuf[p, t] = g_ref[first + t]

        loop(0, n, keep)

        @pl.when(p == 0)
        def _():
            def use(t):
                g_wait(1, t)
                add_h(1, gbuf[1, t], l_ref[first + t])

            loop(0, cut, use)

        @pl.when(p == 1)
        def _():
            def fill(t):
                gbuf[0, t] = g_ref[first + t]

            loop(0, cut, fill)

            def use(t):
                g_wait(0, t)
                add_h(1, g_ref[first + t], gbuf[0, t])

            loop(cut, n, use)

        h_mate(1).start()
        reduce_mate(1)

        @pl.when(top)
        def _():
            reduce_root(1)

        @pl.when(p == 1)
        def _():
            loop(cut, n, cross_hi)

        @pl.when(p == 0)
        def _():
            put_x(0, -w[0])
            put_x(1, -w[2])

        @pl.when(p == 1)
        def _():
            xh[0] = jnp.zeros((tile, tile), BF16)
            xl[0] = jnp.zeros((tile, tile), BF16)
            put_x(1, -w[1])

        @pl.when(jnp.logical_not(top))
        def _():
            own[...] = jnp.zeros((tile, tile), F32)

        @pl.when(top)
        def _():
            rdma(htwin.at[0], htwin.at[0], hs.at[0, 2], hr.at[0, 1], {"col": twin}).wait_recv()
            rdma(htwin.at[1], htwin.at[1], hs.at[1, 2], hr.at[1, 1], {"col": twin}).wait_recv()
            mine, theirs = hsum[0], htwin[0]
            hfull[0, c] = jnp.where(p == 0, mine, theirs)
            hfull[2, c] = jnp.where(p == 0, theirs, mine)
            hfull[1, c] = hsum[1] + htwin[1]
            for k in range(3):
                h_full(k).start()
            for k in range(3):
                rdma(
                    hfull.at[k, 1 - c], hfull.at[k, 1 - c], hs.at[k, 3], hr.at[k, 2], {"row": mate}
                ).wait_recv()

            def d_wait(k):
                rdma(gd.at[k], gd.at[k], ds.at[0], dr.at[k], {"row": mate}).wait_recv()

            @pl.when(jnp.logical_not((c == 1) & (p == 1)))
            def _():
                d_wait(2)

            @pl.when(c == 0)
            def _():
                d_wait(1)

            eye = (rows == cols).astype(F32)

            def low(x):
                return jnp.where(rows >= cols, x, 0.0)

            w66, w77, w76 = w[0], w[1], w[2]
            l77 = lbuf[1, 1].astype(F32)

            def full(k):
                return hfull[k].reshape(tile, tile)

            q77 = low(gd[2].astype(F32) - dot3(w77, full(2), 0, 0))
            m77 = dot3(l77, q77, 0, 0)
            phi77 = low(m77) - 0.5 * m77 * eye

            def put_s(s, o):
                sbuf[p] = s.reshape(CHUNKS, tile // CHUNKS, tile)
                own[...] = o

            def tri(s):
                return low(s) - 0.5 * s * eye

            @pl.when((c == 1) & (p == 1))
            def _():
                half77 = dot3(dot3(w77, phi77, 0, 0), w77)
                s = half77 + half77.T
                put_s(s, tri(s))

            @pl.when(jnp.logical_not((c == 1) & (p == 1)))
            def _():
                g76 = jnp.where(c == 1, g_ref[loc].astype(F32), gd[1].astype(F32))
                q76 = g76 - dot3(w77, full(1), 0, 0)
                phi76 = dot3(l77, q76, 0, 0)

                @pl.when((c == 0) & (p == 0))
                def _():
                    t66 = dot3(w66, full(0), 0, 0) + dot3(w76, full(1), 0, 0)
                    q66 = low(g_ref[loc].astype(F32) - t66)
                    m66 = dot3(lbuf[0, 0].astype(F32), q66, 0, 0) + dot3(lbuf[0, 1].astype(F32), q76, 0, 0)
                    phi66 = low(m66) - 0.5 * m66 * eye
                    inner = dot3(phi76, w66) + dot3(phi77, w76)
                    half66 = dot3(w66, dot3(phi66, w66), 0, 0) + dot3(w76, inner, 0, 0)
                    s = half66 + half66.T
                    put_s(s, tri(s))

                @pl.when(jnp.logical_not((c == 0) & (p == 0)))
                def _():
                    inner = dot3(phi76, w66) + dot3(phi77 + phi77.T, w76)

                    @pl.when(c == 1)
                    def _():
                        s = dot3(w77, inner, 0, 0)
                        put_s(s, s)

                    @pl.when(c == 0)
                    def _():
                        put_s(dot3(inner, w77, 0, 0), jnp.zeros((tile, tile), F32))

            if ring > 1:
                loop(0, CHUNKS, lambda k: s_down(k).start())

        @pl.when(p == 0)
        def _():
            loop(cut, n, lambda t: g_wait(1, t))
            loop(cut, n, lambda t: f_cross(t).wait_send())
            for i in range(2):
                if ring > 1:
                    l_down(i, lk.at[i]).wait_send()
                l_cross(i, lk.at[i]).wait_send()

            @pl.when(top & (c == 1))
            def _():
                d_mate(1).wait_send()
                d_diag(1).wait_send()

        @pl.when(p == 1)
        def _():
            loop(0, n, lambda t: g_cross(t, g_ref.at[first + t]).wait_send())
            if ring > 1:
                l_down(1, lk.at[1]).wait_send()
            l_cross(1, lk.at[1]).wait_send()

            @pl.when(top & (c == 1))
            def _():
                d_mate(2).wait_send()
                d_twin(2).wait_send()
                d_diag(2).wait_send()

        if ring > 1:
            loop(0, n, lambda t: g_down(t, g_ref.at[first + t]).wait_send())
        for k in range(2):
            h_mate(k).wait_send()

            @pl.when(jnp.logical_not(top))
            def _():
                h_root(k).wait_send()

            @pl.when(top)
            def _():
                h_twin(k).wait_send()

        @pl.when(top)
        def _():
            for k in range(3):
                h_full(k).wait_send()
            if ring > 1:
                loop(0, CHUNKS, lambda k: s_down(k).wait_send())

    @pl.when(top)
    def _():
        for k in range(pairs - 1):
            k_star(k).wait_send()
        k_mate(l_ref.at[loc]).wait_send()

    @pl.when(jnp.logical_not(top))
    def _():
        k_mate(lk.at[c]).wait_send()


def panel(factor, grad, n_row, n_col, first):
    rows_here, tile = factor.shape[0], factor.shape[1]
    n = rows_here - first
    half = tile // 2
    pairs = n_row // 2
    vmem = pl.BlockSpec(memory_space=pltpu.VMEM)
    dma = pltpu.SemaphoreType.DMA
    return pl.pallas_call(
        functools.partial(panel_kernel, n_row, n_col),
        out_shape=(
            jax.ShapeDtypeStruct((2, n, tile, tile), BF16),
            jax.ShapeDtypeStruct((2, tile, tile), BF16),
            jax.ShapeDtypeStruct((2, tile, tile), BF16),
            jax.ShapeDtypeStruct((tile, tile), F32),
        ),
        in_specs=[vmem, vmem],
        out_specs=(vmem, vmem, vmem, vmem),
        scratch_shapes=[
            pltpu.VMEM((2, tile, tile), BF16),
            pltpu.VMEM((2, 2, tile, tile), BF16),
            pltpu.VMEM((3, tile, tile), F32),
            pltpu.VMEM((2, 2, half, tile), F32),
            pltpu.VMEM((2, tile, tile), F32),
            pltpu.VMEM((tile, tile), F32),
            pltpu.VMEM((pairs, tile, tile), F32),
            pltpu.VMEM((2, half, tile), F32),
            pltpu.VMEM((2, half, tile), F32),
            pltpu.VMEM((2, pairs, half, tile), F32),
            pltpu.VMEM((2, half, tile), F32),
            pltpu.VMEM((3, 2, half, tile), F32),
            pltpu.VMEM((3, tile, tile), BF16),
            pltpu.VMEM((2, CHUNKS, tile // CHUNKS, tile), F32),
            dma((n, 2)),
            dma((2, n)),
            dma((2, 2)),
            dma((2, 2)),
            dma((pairs + 1,)),
            dma((2,)),
            dma((2,)),
            dma((pairs + 1,)),
            dma((3, 4)),
            dma((3, 3 + pairs)),
            dma((3,)),
            dma((3,)),
            dma((CHUNKS, 2)),
            dma((2, CHUNKS)),
        ],
        compiler_params=pltpu.CompilerParams(
            collective_id=0, has_side_effects=True, vmem_limit_bytes=40 * 1024 * 1024
        ),
        name="panel",
    )(factor, grad)


def update_kernel(n_col, first, base_ref, gbuf, xh, xl, own, out_ref):
    tile = base_ref.shape[1]
    lane = out_ref.shape[1]
    parts = tile // lane
    step = pl.program_id(0)
    right = lax.axis_index("col") >= n_col - 2

    def store(i, value):
        for b in range(parts):
            out_ref[pl.ds(i * tile * parts + b, tile, stride=parts), :] = value[:, b * lane : (b + 1) * lane]

    def base(i):
        return jnp.where(right, 0.0, base_ref[i].astype(F32))

    @pl.when(step == 0)
    def _():
        for i in range(first - 1):
            store(i, base(i))
        store(first - 1, own[...])

    @pl.when(step > 0)
    def _():
        for i in range(first):
            total = base(i)
            for part in (xl, xh):
                for s in range(2):
                    total = total - jnp.dot(gbuf[s, i], part[s], preferred_element_type=F32)
            store(i, total)


def update(grad, gbuf, xh, xl, own, n_col, first):
    rows_here, tile = grad.shape[0], grad.shape[1]
    lane = 128
    whole = lambda k: pl.BlockSpec((2, tile, tile), lambda a: (0, 0, 0))
    return pl.pallas_call(
        functools.partial(update_kernel, n_col, first),
        grid=(rows_here // first,),
        out_shape=jax.ShapeDtypeStruct((rows_here * tile * tile // lane, lane), F32),
        in_specs=[
            pl.BlockSpec((first, tile, tile), lambda a: (a, 0, 0)),
            pl.BlockSpec((2, first, tile, tile), lambda a: (0, jnp.maximum(a - 1, 0), 0, 0)),
            whole(0),
            whole(1),
            pl.BlockSpec((tile, tile), lambda a: (0, 0)),
        ],
        out_specs=pl.BlockSpec((first * tile * tile // lane, lane), lambda a: (a, 0)),
        name="update",
    )(grad, gbuf, xh, xl, own)


def per_device(l_saved, l_grad):
    rows_here, tile = l_saved.shape[0], l_saved.shape[2]
    n_row = lax.axis_size("row")
    n_col = lax.axis_size("col")
    assert n_col % n_row == 0 and n_row % 2 == 0
    first = n_col // n_row
    assert rows_here % first == 0
    factor = l_saved.reshape(rows_here, tile, tile)
    grad = l_grad.reshape(rows_here, tile, tile)
    gbuf, xh, xl, own = panel(factor, grad, n_row, n_col, first)
    out = update(grad, gbuf, xh, xl, own, n_col, first)
    return out.reshape(l_grad.shape)


def solution(mesh):
    spec = P(None, "row", None, "col", None)
    return jax.shard_map(
        per_device, mesh=mesh, in_specs=(spec, spec), out_specs=spec, check_vma=False
    )
```

time: 245 us -> 92.9 us (0.38)
  waiting for transfers between devices: 72.8 us -> 0 us
  matrix products: 29.6 us -> 0 us
  blocking collectives: 17.5 us -> 0 us
  between operations: 14 us -> 0.02 us
  other arithmetic: 11.4 us -> 0 us
  local copies, waits for them, and re-layouts: 18.1 us -> 7.06 us
  Pallas kernels: 79.7 us -> 85.5 us
    psum x2 -> x0, waiting for transfers between devices: 72.8 us -> none  [the longest x1 70.1 us: per_device(): lax.psum(jnp.concatenate([jnp.where(my_col == lo, q_mine, z2), jnp.where(...]
    dot_general x28 -> x0, matrix products: 29.6 us -> none  [the longest x8 11.4 us: dot3(): lax.dot_general(a, b, (((ca,), (cb,)), ((), ())), precision=HIGH3, prefer...]
    all_gather x2 -> x0, blocking collectives: 17.5 us -> none  [the longest x1 10.2 us: per_device(): lax.all_gather(grad[loc], 'row')[n_row - 2:].reshape(2 * tile, tile)]
    slice x9 -> x0, local copies, waits for them, and re-layouts: 7.52 us -> none  [the longest x1 3.03 us: per_device(): below_l = factor[first:].reshape(-1, tile)]
    reshape x1 -> x0, local copies, waits for them, and re-layouts: 6.33 us -> none  [per_device(): return out.reshape(l_grad.shape)]
    pallas_call x1 -> x2, Pallas kernels: 79.7 us -> 85.5 us  [the longest x1 77.3 us: panel(): pl.pallas_call(functools.partial(panel_kernel, n_row, n_col), out_shape=(...]
    unnamed x44 -> x12, local copies, waits for them, and re-layouts: 2.82 us -> 7.06 us
    sub x2 -> x0, other arithmetic: 3.9 us -> none  [the longest x1 2.26 us: per_device(): low = base - prod.reshape(-1, tile, tile)]
  transfers between devices with their start and end apart: 2 -> 0, of which waited for: 2 -> 0; matrix products, arithmetic and copies ran while one was open for 12% -> 0% of each run, Pallas kernels for 0% -> 0%
where the time goes in v1:
time: 92.9 us; the launch traced here: 92.6 us
  Pallas kernels  85.5 us (92%)
  local copies, waits for them, and re-layouts  7.06 us (8%)
    pallas_call x1, Pallas kernels, panel(): pl.pallas_call(functools.partial(panel_kernel, n_row, n_col), out_shape=(...  77.3 us
    pallas_call x1, Pallas kernels, update(): pl.pallas_call(functools.partial(update_kernel, n_col, first), grid=(rows...  8.24 us
    unnamed x12, local copies, waits for them, and re-layouts  7.06 us

profile of v1, /device:TPU:5, one launch (start us, length us, event | category | flops | bytes accessed | tf_op | source)
XLA Modules:
  0.0 92.6 jit_solution(17299600321455131838)
XLA Ops:
  0.0 0.0 copy-start
  0.0 1.6 %copy-done = bf16[16,1,256,1,256]{4,2,3,1,0:T(8,128)(2,1)S(1)} copy-done((bf16[16,1,256,1,256]{4,2,3,1,0:T(8,128)(2,1)S(1)}, bf16[16,1,256,1,256]{4,2,3,1,0:T(8,128)(2,1)}, u32[]{:S(2)}) %copy-start) | copy-done | bytes 2097176
  1.6 0.0 copy-start.2
  1.6 1.6 %copy-done.2 = bf16[16,1,256,1,256]{4,2,3,1,0:T(8,128)(2,1)S(1)} copy-done((bf16[16,1,256,1,256]{4,2,3,1,0:T(8,128)(2,1)S(1)}, bf16[16,1,256,1,256]{4,2,3,1,0:T(8,128)(2,1)}, u32[]{:S(2)}) %copy-start.2) | copy-done | bytes 2097176
  3.2 77.3 %panel.1 = (bf16[2,14,256,256]{3,2,1,0:T(8,128)(2,1)S(1)}, bf16[2,256,256]{2,1,0:T(8,128)(2,1)S(1)}, bf16[2,256,256]{2,1,0:T(8,128)(2,1)S(1)}, f32[256,256]{1,0:T(8,128)S(1)}) custom-call(bf16[16,256,256]{2,1,0:T(8,128)(2,1)S(1)} %bitcast.5, bf16[16,256,256]{2,1,0:T(8,128)(2,1)S(1)} %bitcast.4), custom_call_target="tpu_custom_call" | custom-call | tf_op jit(solution)/shard_map/panel/pallas_call | solution.py:708
  80.5 0.0 copy-start.1
  80.5 1.8 %copy-done.1 = bf16[2,14,256,256]{3,2,1,0:T(8,128)(2,1)} copy-done((bf16[2,14,256,256]{3,2,1,0:T(8,128)(2,1)}, bf16[2,14,256,256]{3,2,1,0:T(8,128)(2,1)S(1)}, u32[]{:S(2)}) %copy-start.1) | copy-done | bytes 3670040
  82.2 0.0 copy-start.3
  82.2 0.7 copy-done.3
  82.9 0.0 copy-start.4
  82.9 0.7 copy-done.4
  83.6 0.0 copy-start.5
  83.6 0.7 copy-done.5
  84.3 8.2 %update.1 = f32[8192,128]{1,0:T(8,128)} custom-call(bf16[16,256,256]{2,1,0:T(8,128)(2,1)} %bitcast.3, bf16[2,14,256,256]{3,2,1,0:T(8,128)(2,1)} %copy-done.1, bf16[2,256,256]{2,1,0:T(8,128)(2,1)} %copy-done.3, bf16[2,256,256]{2,1,0:T(8,128)(2,1)} %copy-done.4, f32[256,256]{1,0:T(8,128)} %copy-done.5), custom_call_target="tpu_custom_call" | custom-call | tf_op jit(solution)/shard_map/update/pallas_call | solution.py:789
Async XLA Ops:
  0.0 1.6 %copy-start = (bf16[16,1,256,1,256]{4,2,3,1,0:T(8,128)(2,1)S(1)}, bf16[16,1,256,1,256]{4,2,3,1,0:T(8,128)(2,1)}, u32[]{:S(2)}) copy-start(bf16[16,1,256,1,256]{4,2,3,1,0:T(8,128)(2,1)} %param.3) | copy-start | bytes 6291460
  1.6 1.6 %copy-start.2 = (bf16[16,1,256,1,256]{4,2,3,1,0:T(8,128)(2,1)S(1)}, bf16[16,1,256,1,256]{4,2,3,1,0:T(8,128)(2,1)}, u32[]{:S(2)}) copy-start(bf16[16,1,256,1,256]{4,2,3,1,0:T(8,128)(2,1)} %param.2) | copy-start | bytes 6291460
  80.5 1.8 %copy-start.1 = (bf16[2,14,256,256]{3,2,1,0:T(8,128)(2,1)}, bf16[2,14,256,256]{3,2,1,0:T(8,128)(2,1)S(1)}, u32[]{:S(2)}) copy-start(bf16[2,14,256,256]{3,2,1,0:T(8,128)(2,1)S(1)} %get-tuple-element.9.gbuf) | copy-start | bytes 11010052
  82.2 0.7 copy-start.3
  82.9 0.7 copy-start.4
  83.6 0.7 copy-start.5

commit v2 on v1

v2 whole, which is shorter than its diff:
```python
import functools

import jax
import jax.numpy as jnp
from jax import lax
from jax.experimental import pallas as pl
from jax.experimental.pallas import tpu as pltpu
from jax.sharding import PartitionSpec as P

F32 = jnp.float32
BF16 = jnp.bfloat16
HIGH3 = lax.Precision.HIGH
MESH = pl.DeviceIdType.MESH
CHUNKS = 8
SUB = 4
LANE = 128
VMEM = 40 * 1024 * 1024


def dot3(a, b, ca=1, cb=0):
    return lax.dot_general(
        a, b, (((ca,), (cb,)), ((), ())), precision=HIGH3, preferred_element_type=F32
    )


def outer(a, b):
    return lax.dot_general(a, b, (((0,), (0,)), ((), ())), preferred_element_type=F32)


def panel_kernel(
    n_row,
    n_col,
    l_hbm,
    g_hbm,
    lin,
    lv,
    gv,
    gbuf,
    xh,
    xl,
    lk,
    lbuf,
    w,
    h,
    tout,
    tin,
    tslot,
    hin,
    hsum,
    hslot,
    htwin,
    hfull,
    gd,
    sbuf,
    vs,
    gs,
    gr,
    ls,
    lr,
    ks,
    kr,
    ts,
    tr,
    hs,
    hr,
    ds,
    dr,
    ss,
    sr,
):
    held, tile = lv.shape[0], lv.shape[3]
    half = tile // 2
    n = gbuf.shape[1]
    first = held - n
    loc = first - 1
    ring = n_col // 2
    cut = n // 2
    head = min(2, n)
    pairs = n_row // 2
    parts = tile // LANE

    row = lax.axis_index("row")
    col = lax.axis_index("col")
    q, p = col // 2, col % 2
    y, c = row // 2, row % 2
    panel = q == ring - 1
    top = y == pairs - 1
    below = q > 0
    lower = jnp.maximum(col - 2, 0)
    twin = 2 * q + 1 - p
    mate = 2 * y + 1 - c
    root = n_row - 2 + c

    rows = lax.broadcasted_iota(jnp.int32, (tile, tile), 0)
    cols = lax.broadcasted_iota(jnp.int32, (tile, tile), 1)

    def rdma(src, dst, s_sem, r_sem, dev):
        return pltpu.make_async_remote_copy(
            src_ref=src, dst_ref=dst, send_sem=s_sem, recv_sem=r_sem, device_id=dev, device_id_type=MESH
        )

    def loop(a, b, body):
        def step(i, carry):
            body(i)
            return carry

        if a < b:
            lax.fori_loop(a, b, step, 0)

    def load(src, dst, k, a, b):
        return pltpu.make_async_copy(src.at[pl.ds(a, b - a)], dst.at[pl.ds(a, b - a)], vs.at[k])

    spans = [
        (l_hbm, lv, 0, loc, first),
        (g_hbm, gv, 1, first, first + head),
        (l_hbm, lv, 2, first, held),
        (g_hbm, gv, 3, first + head, held),
        (g_hbm, gv, 4, 0, first),
    ]
    loads = [load(*span) for span in spans if span[3] < span[4]]
    for cp in loads:
        cp.start()

    barrier = pltpu.get_barrier_semaphore()

    def greet(dev):
        pl.semaphore_signal(barrier, inc=1, device_id=dev, device_id_type=MESH)

    greet({"col": twin})
    greet({"row": mate})

    @pl.when(below)
    def _():
        greet({"col": col - 2})

    @pl.when(jnp.logical_not(panel))
    def _():
        greet({"col": col + 2})

    @pl.when(jnp.logical_not(top))
    def _():
        greet({"row": root})

    @pl.when(top)
    def _():
        for k in range(pairs - 1):
            greet({"row": 2 * k + c})

    @pl.when(top & panel)
    def _():
        greet({"row": mate, "col": twin})

    heard = (
        2
        + below.astype(jnp.int32)
        + jnp.logical_not(panel).astype(jnp.int32)
        + jnp.where(top, pairs - 1, 1)
        + (top & panel).astype(jnp.int32)
    )
    with jax.named_scope("barrier"):
        pl.semaphore_wait(barrier, heard)

    with jax.named_scope("loads"):
        for cp in loads:
            cp.wait()

    def mat(ref, *at):
        return ref[at].reshape(tile, tile)

    def g_down(t, k, src):
        return rdma(src.at[k], gbuf.at[p, t, k], gs.at[t, k, 0], gr.at[p, t, k], {"col": lower})

    def g_cross(t, k, src):
        return rdma(src.at[k], gbuf.at[p, t, k], gs.at[t, k, 1], gr.at[p, t, k], {"col": twin})

    def g_wait(s, t, k):
        ref = gbuf.at[s, t, k]
        rdma(ref, ref, gs.at[t, k, 0], gr.at[s, t, k], {"col": twin}).wait_recv()

    def f_cross(t, k):
        return rdma(lv.at[first + t, k], gbuf.at[0, t, k], gs.at[t, k, 1], gr.at[0, t, k], {"col": twin})

    def l_down(k, src):
        return rdma(src.at[k], lbuf.at[p, c, k], ls.at[p, k, 0], lr.at[p, c, k], {"col": lower})

    def l_cross(k, src):
        return rdma(src.at[k], lbuf.at[p, c, k], ls.at[p, k, 1], lr.at[p, c, k], {"col": twin})

    def l_mate(s, k):
        ref = lbuf.at[s, c, k]
        return rdma(ref, ref, ls.at[s, k, 2], lr.at[s, c, k], {"row": mate})

    def l_wait(s, i, k):
        ref = lbuf.at[s, i, k]
        rdma(ref, ref, ls.at[s, k, 2], lr.at[s, i, k], {"row": mate}).wait_recv()

    def k_star(k):
        return rdma(lv.at[loc], lk.at[c], ks.at[k], kr.at[c], {"row": 2 * k + c})

    def k_mate(src):
        return rdma(src, lk.at[c], ks.at[pairs], kr.at[c], {"row": mate})

    def k_wait(i):
        rdma(lk.at[i], lk.at[i], ks.at[pairs], kr.at[i], {"row": mate}).wait_recv()

    def t_mate():
        return rdma(tout.at[1 - c], tin, ts.at[0], tr.at[pairs], {"row": mate})

    def t_root():
        return rdma(tout.at[c], tslot.at[y], ts.at[1], tr.at[y], {"row": root})

    def h_mate(k):
        return rdma(h.at[k, 1 - c], hin.at[k], hs.at[k, 0], hr.at[k, 0], {"row": mate})

    def h_root(k):
        return rdma(hsum.at[k], hslot.at[k, y], hs.at[k, 1], hr.at[k, 3 + y], {"row": root})

    def h_twin(k):
        return rdma(hsum.at[k], htwin.at[k], hs.at[k, 2], hr.at[k, 1], {"col": twin})

    def h_full(k):
        return rdma(hfull.at[k, c], hfull.at[k, c], hs.at[k, 3], hr.at[k, 2], {"row": mate})

    def d_copy(k, src, i, dev):
        return rdma(src, gd.at[k], ds.at[i], dr.at[k], dev)

    def d_wait(k):
        d_copy(k, gd.at[k], 0, {"row": mate}).wait_recv()

    def s_down(k):
        return rdma(sbuf.at[p, k], sbuf.at[p, k], ss.at[k, 0], sr.at[p, k], {"col": lower})

    def s_cross(k):
        return rdma(sbuf.at[p, k], sbuf.at[p, k], ss.at[k, 1], sr.at[p, k], {"col": twin})

    def s_wait(s, k):
        rdma(sbuf.at[s, k], sbuf.at[s, k], ss.at[k, 0], sr.at[s, k], {"col": twin}).wait_recv()

    @pl.when(top)
    def _():
        for k in range(pairs - 1):
            k_star(k).start()
        k_mate(lv.at[loc]).start()
        lk[c] = lv[loc]

    def gather_rows():
        @pl.when(jnp.logical_not(top))
        def _():
            k_wait(c)
            k_mate(lk.at[c]).start()

        k_wait(1 - c)

    def start_inverse(k):
        d = mat(lbuf, k, k).astype(F32)
        e = (rows == cols).astype(F32)
        on = d * e
        rc = 1.0 / jnp.sum(on, axis=1, keepdims=True)
        rr = 1.0 / jnp.sum(on, axis=0, keepdims=True)
        off = ((rows & 1) == 1) & (cols == rows - 1)
        w[k] = e * rr - rc * jnp.where(off, d, 0.0) * rr

    n_lev = tile.bit_length() - 2

    def inverse_level(sh, k):
        off = ((jnp.right_shift(rows, sh) & 1) == 1) & (
            jnp.right_shift(cols, sh) == jnp.right_shift(rows, sh) - 1
        )
        part = jnp.where(off, mat(lbuf, k, k).astype(F32), 0.0)
        cur = w[k]
        w[k] = cur - dot3(cur, dot3(part, cur))

    def finish_inverse():
        w[2] = -dot3(w[1], dot3(mat(lbuf, 0, 1).astype(F32), w[0]))

    def put_x(i, x):
        hi = x.astype(BF16)
        xh[i] = hi
        xl[i] = (x - hi.astype(F32)).astype(BF16)

    def store(a, value):
        for b in range(parts):
            lin[a, pl.ds(b, tile, stride=parts), :] = value[:, b * LANE : (b + 1) * LANE]

    h[...] = jnp.zeros_like(h)

    def add_h(k, left, right):
        h[k] += outer(left, right).reshape(2, half, tile)

    def times_x(total, i, g):
        for part in (xl, xh):
            total = total - jnp.dot(g, part[i], preferred_element_type=F32)
        return total

    @pl.when(jnp.logical_not(panel))
    def _():
        def relay(t, work=()):
            for k in range(SUB):
                with jax.named_scope("w_main"):
                    g_wait(p, t, k)

                @pl.when(below)
                def _():
                    g_down(t, k, gbuf.at[p, t]).start()

                g_cross(t, k, gbuf.at[p, t]).start()
                if k < len(work):
                    work[k]()

        def use(t):
            with jax.named_scope("w_cross"):
                for k in range(SUB):
                    g_wait(1 - p, t, k)
            right = mat(lv, first + t)
            add_h(0, mat(gbuf, 0, t), right)
            add_h(1, mat(gbuf, 1, t), right)

        def low(t):
            total = mat(gv, first + t).astype(F32)
            for s in range(2):
                total = times_x(total, s, mat(gbuf, s, t))
            store(first + t, total)

        main_l = (p == 0) | (c == 1)
        other_l = (p == 1) | (c == 1)

        for t in range(head):
            relay(t)
        with jax.named_scope("gather"):
            gather_rows()

        with jax.named_scope("l_relay"):

            @pl.when(main_l)
            def _():
                def step(k):
                    l_wait(p, c, k)

                    @pl.when(below)
                    def _():
                        l_down(k, lbuf.at[p, c]).start()

                    l_cross(k, lbuf.at[p, c]).start()
                    l_mate(p, k).start()

                loop(0, SUB, step)

        if n > head:
            relay(head)
        with jax.named_scope("l_wait"):

            @pl.when(other_l)
            def _():
                def step(k):
                    l_wait(1 - p, c, k)
                    l_mate(1 - p, k).start()

                loop(0, SUB, step)

            loop(0, SUB, lambda k: l_wait(0, 1 - c, k))

            @pl.when(c == 0)
            def _():
                loop(0, SUB, lambda k: l_wait(1, 1, k))

        start_inverse(0)
        start_inverse(1)
        if n > head + 1:
            use(0)

        base = min(head + 1, n)
        inside = min(n_lev, n - base)

        def level_step(i):
            lev = i - base + 1
            relay(
                i,
                (
                    lambda: inverse_level(lev, 0),
                    lambda: inverse_level(lev, 1),
                    lambda: use(i - 2),
                ),
            )

        loop(base, base + inside, level_step)

        def level_rest(lev):
            inverse_level(lev, 0)
            inverse_level(lev, 1)

        loop(inside + 1, n_lev + 1, level_rest)

        def x_first():
            put_x(0, dot3(w[0], mat(lk, 0).astype(F32)))

        def x_second():
            put_x(1, dot3(w[2], mat(lk, 0).astype(F32)) + dot3(w[1], mat(lk, 1).astype(F32)))

        at = base + inside
        if at < n:
            relay(at, (finish_inverse, x_first, x_second, lambda: use(at - 2)))
            at += 1
        else:
            finish_inverse()
            x_first()
            x_second()
        begun = at

        per = 3 if n <= begun + 4 else 1

        def low_step(i):
            j = (i - begun) * per
            relay(i, [functools.partial(lambda d: low(j + d), d) for d in range(per)] + [lambda: use(i - 2)])

        loop(begun, n, low_step)
        lows = per * max(n - begun, 0)
        used = max(n - 2, 0) if n > base else 0

        def send_t():
            loop(used, n, use)
            h0, h1 = mat(h, 0), mat(h, 1)
            tout[1] = dot3(w[1], h1, 0, 0)
            tout[0] = dot3(w[0], h0, 0, 0) + dot3(w[2], h1, 0, 0)
            t_mate().start()

        def upper(a):
            store(a, mat(gv, a).astype(F32))

        @pl.when(jnp.logical_not(top))
        def _():
            send_t()
            with jax.named_scope("w_tmate"):
                t_mate().wait_recv()
            tout[c] += tin[...]
            t_root().start()
            loop(lows, n, low)
            loop(0, loc + 1, upper)

        @pl.when(top)
        def _():
            def s_relay(k):
                with jax.named_scope("w_s"):
                    s_wait(p, k)

                @pl.when(below)
                def _():
                    s_down(k).start()

                s_cross(k).start()

            loop(0, CHUNKS, s_relay)
            send_t()
            loop(lows, n, low)
            loop(0, loc, upper)
            with jax.named_scope("w_s2"):
                loop(0, CHUNKS, lambda k: s_wait(1 - p, k))
            k0, k1 = mat(lk, 0).astype(F32), mat(lk, 1).astype(F32)
            total = mat(gv, loc).astype(F32) - dot3(mat(sbuf, 0), k0) - dot3(mat(sbuf, 1), k1)
            with jax.named_scope("w_tmate2"):
                t_mate().wait_recv()
            total = total - (tout[c] + tin[...])
            with jax.named_scope("w_tslot"):
                for k in range(pairs - 1):
                    rdma(tslot.at[k], tslot.at[k], ts.at[1], tr.at[k], {"row": mate}).wait_recv()
            for k in range(pairs - 1):
                total = total - tslot[k]
            store(loc, total)

        drain = jax.named_scope("drain")
        drain.__enter__()

        def drain_g(t):
            for k in range(SUB):

                @pl.when(below)
                def _():
                    g_down(t, k, gbuf.at[p, t]).wait_send()

                g_cross(t, k, gbuf.at[p, t]).wait_send()

        loop(0, n, drain_g)

        @pl.when(main_l)
        def _():
            def step(k):
                @pl.when(below)
                def _():
                    l_down(k, lbuf.at[p, c]).wait_send()

                l_cross(k, lbuf.at[p, c]).wait_send()
                l_mate(p, k).wait_send()

            loop(0, SUB, step)

        @pl.when(other_l)
        def _():
            loop(0, SUB, lambda k: l_mate(1 - p, k).wait_send())

        t_mate().wait_send()

        @pl.when(jnp.logical_not(top))
        def _():
            t_root().wait_send()

        @pl.when(top)
        def _():
            def drain_s(k):
                @pl.when(below)
                def _():
                    s_down(k).wait_send()

                s_cross(k).wait_send()

            loop(0, CHUNKS, drain_s)

        drain.__exit__(None, None, None)

    @pl.when(panel)
    def _():
        def each(body):
            def run(t):
                for k in range(SUB):
                    body(t, k)

            return run

        send = each(lambda t, k: g_down(t, k, gv.at[first + t]).start() if ring > 1 else None)
        cross_lo = each(lambda t, k: f_cross(t, k).start())
        cross_hi = each(lambda t, k: g_cross(t, k, gv.at[first + t]).start())
        lead = min(2, cut)
        mid = min(cut + 2, n)
        loop(0, head, send)

        @pl.when(p == 0)
        def _():
            loop(cut, mid, cross_lo)

        @pl.when(p == 1)
        def _():
            loop(0, lead, cross_hi)

        with jax.named_scope("gather"):
            gather_rows()

        def send_l():
            def step(k):
                if ring > 1:
                    l_down(k, lk.at[c]).start()
                l_cross(k, lk.at[c]).start()

            loop(0, SUB, step)

        @pl.when(p == 0)
        def _():
            send_l()
            lbuf[0] = lk[...]
            loop(mid, n, cross_lo)

            @pl.when(top & (c == 1))
            def _():
                d_copy(1, gv.at[loc], 0, {"row": mate}).start()
                d_copy(1, gv.at[loc], 1, {"row": mate, "col": twin}).start()
                gd[1] = gv[loc]

        @pl.when(p == 1)
        def _():
            @pl.when(c == 1)
            def _():
                send_l()

            lbuf[1, 1] = lk[1]
            loop(lead, cut, cross_hi)

            @pl.when(top & (c == 1))
            def _():
                d_copy(2, gv.at[loc], 0, {"row": mate}).start()
                d_copy(2, gv.at[loc], 1, {"col": twin}).start()
                gd[2] = gv[loc]

        loop(head, n, send)

        with jax.named_scope("hd"):
            loop(0, n, lambda t: add_h(0, mat(gv, first + t), mat(lv, first + t)))
        h_mate(0).start()

        with jax.named_scope("l_wait"):
            @pl.when((p == 1) | (c == 1))
            def _():
                def step(k):
                    l_wait(1 - p, c, k)
                    l_mate(1 - p, k).start()

                loop(0, SUB, step)

            @pl.when(p == 1)
            def _():
                loop(0, SUB, lambda k: l_wait(0, 1 - c, k))

            @pl.when((p == 0) & (c == 0))
            def _():
                loop(0, SUB, lambda k: l_wait(1, 1, k))

        def reduce_mate(k):
            with jax.named_scope("w_hmate"):
                h_mate(k).wait_recv()
            hsum[k] = h[k, c] + hin[k]

            @pl.when(jnp.logical_not(top))
            def _():
                h_root(k).start()

        def reduce_root(k):
            total = hsum[k]
            for i in range(pairs - 1):
                with jax.named_scope("w_hroot"):
                    rdma(
                        hslot.at[k, i], hslot.at[k, i], hs.at[k, 1], hr.at[k, 3 + i], {"row": mate}
                    ).wait_recv()
                total = total + hslot[k, i]
            hsum[k] = total
            h_twin(k).start()

        start_inverse(0)
        start_inverse(1)
        reduce_mate(0)

        def level(lev):
            inverse_level(lev, 0)
            inverse_level(lev, 1)

        early = (n_lev + 1) // 2
        loop(1, early + 1, level)

        @pl.when(top)
        def _():
            reduce_root(0)

        loop(early + 1, n_lev + 1, level)
        finish_inverse()

        def g_whole(s, t):
            with jax.named_scope("w_x"):
                for k in range(SUB):
                    g_wait(s, t, k)

        @pl.when(p == 0)
        def _():
            def use(t):
                g_whole(1, t)
                add_h(1, mat(gbuf, 1, t), mat(lv, first + t))

            loop(0, cut, use)

        @pl.when(p == 1)
        def _():
            def use(t):
                g_whole(0, t)
                add_h(1, mat(gv, first + t), mat(gbuf, 0, t))

            loop(cut, n, use)

        h_mate(1).start()

        @pl.when(top & (c == 1) & (p == 0))
        def _():
            d_wait(2)
            d_copy(2, gd.at[2], 2, {"row": mate}).start()

        reduce_mate(1)

        @pl.when(top)
        def _():
            reduce_root(1)

        @pl.when(p == 1)
        def _():
            loop(cut, n, cross_hi)

        @pl.when(top)
        def _():
            with jax.named_scope("w_htwin"):
                for k in range(2):
                    rdma(htwin.at[k], htwin.at[k], hs.at[k, 2], hr.at[k, 1], {"col": twin}).wait_recv()
            mine, theirs = hsum[0], htwin[0]
            hfull[0, c] = jnp.where(p == 0, mine, theirs)
            hfull[2, c] = jnp.where(p == 0, theirs, mine)
            hfull[1, c] = hsum[1] + htwin[1]
            for k in range(3):
                h_full(k).start()
            with jax.named_scope("w_hfull"):
                for k in range(3):
                    ref = hfull.at[k, 1 - c]
                    rdma(ref, ref, hs.at[k, 3], hr.at[k, 2], {"row": mate}).wait_recv()

                @pl.when(c == 0)
                def _():
                    d_wait(1)
                    d_wait(2)

            eye = (rows == cols).astype(F32)

            def keep(x):
                return jnp.where(rows >= cols, x, 0.0)

            w66, w77, w76 = w[0], w[1], w[2]
            l77 = mat(lbuf, 1, 1).astype(F32)
            g_here = mat(gv, loc).astype(F32)

            q77 = keep(mat(gd, 2).astype(F32) - dot3(w77, mat(hfull, 2), 0, 0))
            m77 = dot3(l77, q77, 0, 0)
            phi77 = keep(m77) - 0.5 * m77 * eye

            def put_s(s, o):
                sbuf[p] = s.reshape(CHUNKS, tile // CHUNKS, tile)
                if ring > 1:
                    loop(0, CHUNKS, lambda k: s_down(k).start())
                store(loc, o)

            def tri(s):
                return keep(s) - 0.5 * s * eye

            @pl.when((c == 1) & (p == 1))
            def _():
                half77 = dot3(dot3(w77, phi77, 0, 0), w77)
                s = half77 + half77.T
                put_s(s, tri(s))

            @pl.when(jnp.logical_not((c == 1) & (p == 1)))
            def _():
                g76 = jnp.where(c == 1, g_here, mat(gd, 1).astype(F32))
                q76 = g76 - dot3(w77, mat(hfull, 1), 0, 0)
                phi76 = dot3(l77, q76, 0, 0)

                @pl.when((c == 0) & (p == 0))
                def _():
                    t66 = dot3(w66, mat(hfull, 0), 0, 0) + dot3(w76, mat(hfull, 1), 0, 0)
                    q66 = keep(g_here - t66)
                    l66, l76 = mat(lbuf, 0, 0).astype(F32), mat(lbuf, 0, 1).astype(F32)
                    m66 = dot3(l66, q66, 0, 0) + dot3(l76, q76, 0, 0)
                    phi66 = keep(m66) - 0.5 * m66 * eye
                    inner = dot3(phi76, w66) + dot3(phi77, w76)
                    half66 = dot3(w66, dot3(phi66, w66), 0, 0) + dot3(w76, inner, 0, 0)
                    s = half66 + half66.T
                    put_s(s, tri(s))

                @pl.when(jnp.logical_not((c == 0) & (p == 0)))
                def _():
                    inner = dot3(phi76, w66) + dot3(phi77 + phi77.T, w76)

                    @pl.when(c == 1)
                    def _():
                        s = dot3(w77, inner, 0, 0)
                        put_s(s, s)

                    @pl.when(c == 0)
                    def _():
                        put_s(dot3(inner, w77, 0, 0), jnp.zeros((tile, tile), F32))

        zero = jnp.zeros((tile, tile), F32)
        loop(0, loc, lambda a: store(a, zero))

        @pl.when(jnp.logical_not(top))
        def _():
            store(loc, zero)

        put_x(1, jnp.where(p == 0, -w[2], -w[1]))

        with jax.named_scope("low"):

            @pl.when(p == 0)
            def _():
                put_x(0, -w[0])

                def low(t):
                    total = times_x(zero, 0, mat(gv, first + t))
                    store(first + t, times_x(total, 1, mat(gbuf, 1, t)))

                def late(t):
                    g_whole(1, t)
                    low(t)

                loop(0, cut, low)
                loop(cut, n, late)

            @pl.when(p == 1)
            def _():
                loop(0, n, lambda t: store(first + t, times_x(zero, 1, mat(gv, first + t))))

        drain = jax.named_scope("drain")
        drain.__enter__()

        def drain_l():
            def step(k):
                if ring > 1:
                    l_down(k, lk.at[c]).wait_send()
                l_cross(k, lk.at[c]).wait_send()

            loop(0, SUB, step)

        @pl.when(p == 0)
        def _():
            loop(cut, n, each(lambda t, k: f_cross(t, k).wait_send()))
            drain_l()

            @pl.when(top & (c == 1))
            def _():
                d_copy(1, gv.at[loc], 0, {"row": mate}).wait_send()
                d_copy(1, gv.at[loc], 1, {"row": mate, "col": twin}).wait_send()
                d_copy(2, gd.at[2], 2, {"row": mate}).wait_send()

        @pl.when(p == 1)
        def _():
            loop(0, n, each(lambda t, k: g_cross(t, k, gv.at[first + t]).wait_send()))

            @pl.when(c == 1)
            def _():
                drain_l()

            @pl.when(top & (c == 1))
            def _():
                d_copy(2, gv.at[loc], 0, {"row": mate}).wait_send()
                d_copy(2, gv.at[loc], 1, {"col": twin}).wait_send()

        @pl.when((p == 1) | (c == 1))
        def _():
            loop(0, SUB, lambda k: l_mate(1 - p, k).wait_send())

        if ring > 1:
            loop(0, n, each(lambda t, k: g_down(t, k, gv.at[first + t]).wait_send()))
        for k in range(2):
            h_mate(k).wait_send()

            @pl.when(jnp.logical_not(top))
            def _():
                h_root(k).wait_send()

            @pl.when(top)
            def _():
                h_twin(k).wait_send()

        @pl.when(top)
        def _():
            for k in range(3):
                h_full(k).wait_send()
            if ring > 1:
                loop(0, CHUNKS, lambda k: s_down(k).wait_send())

        drain.__exit__(None, None, None)

    @pl.when(top)
    def _():
        for k in range(pairs - 1):
            k_star(k).wait_send()
        k_mate(lv.at[loc]).wait_send()

    @pl.when(jnp.logical_not(top))
    def _():
        k_mate(lk.at[c]).wait_send()


def panel(factor, grad, n_row, n_col, first):
    rows_here, tile = factor.shape[0], factor.shape[1]
    n = rows_here - first
    half = tile // 2
    pairs = n_row // 2
    sub = (SUB, tile // SUB, tile)
    hbm = pl.BlockSpec(memory_space=pltpu.HBM)
    dma = pltpu.SemaphoreType.DMA
    return pl.pallas_call(
        functools.partial(panel_kernel, n_row, n_col),
        out_shape=jax.ShapeDtypeStruct((rows_here, tile * tile // LANE, LANE), F32),
        in_specs=[hbm, hbm],
        out_specs=pl.BlockSpec(memory_space=pltpu.VMEM),
        scratch_shapes=[
            pltpu.VMEM((rows_here, *sub), BF16),
            pltpu.VMEM((rows_here, *sub), BF16),
            pltpu.VMEM((2, n, *sub), BF16),
            pltpu.VMEM((2, tile, tile), BF16),
            pltpu.VMEM((2, tile, tile), BF16),
            pltpu.VMEM((2, *sub), BF16),
            pltpu.VMEM((2, 2, *sub), BF16),
            pltpu.VMEM((3, tile, tile), F32),
            pltpu.VMEM((2, 2, half, tile), F32),
            pltpu.VMEM((2, tile, tile), F32),
            pltpu.VMEM((tile, tile), F32),
            pltpu.VMEM((pairs, tile, tile), F32),
            pltpu.VMEM((2, half, tile), F32),
            pltpu.VMEM((2, half, tile), F32),
            pltpu.VMEM((2, pairs, half, tile), F32),
            pltpu.VMEM((2, half, tile), F32),
            pltpu.VMEM((3, 2, half, tile), F32),
            pltpu.VMEM((3, *sub), BF16),
            pltpu.VMEM((2, CHUNKS, tile // CHUNKS, tile), F32),
            dma((5,)),
            dma((n, SUB, 2)),
            dma((2, n, SUB)),
            dma((2, SUB, 3)),
            dma((2, 2, SUB)),
            dma((pairs + 1,)),
            dma((2,)),
            dma((2,)),
            dma((pairs + 1,)),
            dma((3, 4)),
            dma((3, 3 + pairs)),
            dma((3,)),
            dma((3,)),
            dma((CHUNKS, 2)),
            dma((2, CHUNKS)),
        ],
        compiler_params=pltpu.CompilerParams(
            collective_id=0, has_side_effects=True, vmem_limit_bytes=VMEM
        ),
        name="panel",
    )(
        pltpu.with_memory_space_constraint(factor.reshape(rows_here, *sub), pltpu.HBM),
        pltpu.with_memory_space_constraint(grad.reshape(rows_here, *sub), pltpu.HBM),
    )


def per_device(l_saved, l_grad):
    rows_here, tile = l_saved.shape[0], l_saved.shape[2]
    n_row = lax.axis_size("row")
    n_col = lax.axis_size("col")
    assert n_col % n_row == 0 and n_row % 2 == 0 and tile % (SUB * 16) == 0
    first = n_col // n_row
    factor = l_saved.reshape(rows_here, tile, tile)
    grad = l_grad.reshape(rows_here, tile, tile)
    lin = panel(factor, grad, n_row, n_col, first)
    return lin.reshape(l_grad.shape)


def solution(mesh):
    spec = P(None, "row", None, "col", None)
    return jax.shard_map(
        per_device, mesh=mesh, in_specs=(spec, spec), out_specs=spec, check_vma=False
    )
```

time: 92.9 us -> 72.8 us (0.78)
  Pallas kernels: 85.5 us -> 70.7 us
  local copies, waits for them, and re-layouts: 7.06 us -> 2.02 us
    pallas_call x2 -> x1, Pallas kernels: 85.5 us -> 70.7 us  [panel(): pl.pallas_call(functools.partial(panel_kernel, n_row, n_col), out_shape=j...]
    unnamed x12 -> x1, local copies, waits for them, and re-layouts: 7.06 us -> 2.02 us
where the time goes in v2:
time: 72.8 us; the launch traced here: 72.7 us
  Pallas kernels  70.7 us (97%)
  local copies, waits for them, and re-layouts  2.02 us (3%)
    pallas_call x1, Pallas kernels, panel(): pl.pallas_call(functools.partial(panel_kernel, n_row, n_col), out_shape=j...  70.7 us
    unnamed x1, local copies, waits for them, and re-layouts  2.02 us

profile of v2, /device:TPU:5, one launch (start us, length us, event | category | flops | bytes accessed | tf_op | source)
XLA Modules:
  0.0 72.7 jit_solution(12619949642083650090)
XLA Ops:
  0.0 70.7 %panel.1 = f32[16,512,128]{2,1,0:T(8,128)S(1)} custom-call(bf16[16,4,64,256]{3,2,1,0:T(8,128)(2,1)} %bitcast.4, bf16[16,4,64,256]{3,2,1,0:T(8,128)(2,1)} %bitcast.5), custom_call_target="tpu_custom_call" | custom-call | tf_op jit(solution)/shard_map/panel/pallas_call | solution.py:869
  70.7 2.0 %copy.5 = f32[16,1,256,1,256]{4,3,2,1,0:T(1,128)} copy(f32[16,1,256,1,256]{4,3,2,1,0:T(1,128)S(1)} %bitcast.3) | data formatting | bytes 8388608

commit v3 on v2

--- a/solution.py
+++ b/solution.py
@@ -54,19 +54,24 @@
     sbuf,
     vs,
     gs,
-    gr,
+    gm,
+    gx,
     ls,
-    lr,
+    lm,
+    lx,
+    lf,
     ks,
     kr,
     ts,
     tr,
     hs,
     hr,
+    hq,
     ds,
     dr,
     ss,
-    sr,
+    sm,
+    sx,
 ):
     held, tile = lv.shape[0], lv.shape[3]
     half = tile // 2
@@ -117,9 +122,14 @@
         (g_hbm, gv, 3, first + head, held),
         (g_hbm, gv, 4, 0, first),
     ]
-    loads = [load(*span) for span in spans if span[3] < span[4]]
-    for cp in loads:
+    loads = {span[2]: load(*span) for span in spans if span[3] < span[4]}
+    for cp in loads.values():
         cp.start()
+
+    def loaded(*ks):
+        for k in ks:
+            if k in loads:
+                loads[k].wait()
 
     barrier = pltpu.get_barrier_semaphore()
 
@@ -160,39 +170,56 @@
     with jax.named_scope("barrier"):
         pl.semaphore_wait(barrier, heard)
 
-    with jax.named_scope("loads"):
-        for cp in loads:
-            cp.wait()
+    loaded(0)
 
     def mat(ref, *at):
         return ref[at].reshape(tile, tile)
 
     def g_down(t, k, src):
-        return rdma(src.at[k], gbuf.at[p, t, k], gs.at[t, k, 0], gr.at[p, t, k], {"col": lower})
+        return rdma(src.at[k], gbuf.at[p, t, k], gs.at[0], gm.at[t, k], {"col": lower})
 
     def g_cross(t, k, src):
-        return rdma(src.at[k], gbuf.at[p, t, k], gs.at[t, k, 1], gr.at[p, t, k], {"col": twin})
-
-    def g_wait(s, t, k):
-        ref = gbuf.at[s, t, k]
-        rdma(ref, ref, gs.at[t, k, 0], gr.at[s, t, k], {"col": twin}).wait_recv()
+        return rdma(src.at[k], gbuf.at[p, t, k], gs.at[1], gx.at[t], {"col": twin})
 
     def f_cross(t, k):
-        return rdma(lv.at[first + t, k], gbuf.at[0, t, k], gs.at[t, k, 1], gr.at[0, t, k], {"col": twin})
+        return rdma(lv.at[first + t, k], gbuf.at[0, t, k], gs.at[1], gx.at[t], {"col": twin})
+
+    def g_main(t, k):
+        ref = gbuf.at[p, t, k]
+        rdma(ref, ref, gs.at[0], gm.at[t, k], {"col": twin}).wait_recv()
+
+    def g_twin(t):
+        ref = gbuf.at[1 - p, t]
+        rdma(ref, ref, gs.at[1], gx.at[t], {"col": twin}).wait_recv()
+
+    def g_sent(k, ref):
+        rdma(ref, ref, gs.at[k], gx.at[0], {"col": twin}).wait_send()
 
     def l_down(k, src):
-        return rdma(src.at[k], lbuf.at[p, c, k], ls.at[p, k, 0], lr.at[p, c, k], {"col": lower})
+        return rdma(src.at[k], lbuf.at[p, c, k], ls.at[0], lm.at[k], {"col": lower})
 
     def l_cross(k, src):
-        return rdma(src.at[k], lbuf.at[p, c, k], ls.at[p, k, 1], lr.at[p, c, k], {"col": twin})
+        return rdma(src.at[k], lbuf.at[p, c, k], ls.at[1], lx.at[k], {"col": twin})
 
     def l_mate(s, k):
         ref = lbuf.at[s, c, k]
-        return rdma(ref, ref, ls.at[s, k, 2], lr.at[s, c, k], {"row": mate})
-
-    def l_wait(s, i, k):
-        ref = lbuf.at[s, i, k]
-        rdma(ref, ref, ls.at[s, k, 2], lr.at[s, i, k], {"row": mate}).wait_recv()
+        return rdma(ref, ref, ls.at[2 + s], lf.at[s], {"row": mate})
+
+    def l_main(k):
+        ref = lbuf.at[p, c, k]
+        rdma(ref, ref, ls.at[0], lm.at[k], {"col": twin}).wait_recv()
+
+    def l_twin(k):
+        ref = lbuf.at[1 - p, c, k]
+        rdma(ref, ref, ls.at[1], lx.at[k], {"col": twin}).wait_recv()
+
+    def l_full(s):
+        ref = lbuf.at[s, 1 - c]
+        rdma(ref, ref, ls.at[2], lf.at[s], {"row": mate}).wait_recv()
+
+    def l_sent(k):
+        ref = lbuf.at[0, 0]
+        rdma(ref, ref, ls.at[k], lf.at[0], {"row": mate}).wait_send()
 
     def k_star(k):
         return rdma(lv.at[loc], lk.at[c], ks.at[k], kr.at[c], {"row": 2 * k + c})
@@ -210,16 +237,16 @@
         return rdma(tout.at[c], tslot.at[y], ts.at[1], tr.at[y], {"row": root})
 
     def h_mate(k):
-        return rdma(h.at[k, 1 - c], hin.at[k], hs.at[k, 0], hr.at[k, 0], {"row": mate})
+        return rdma(h.at[k, 1 - c], hin.at[k], hs.at[k], hr.at[k], {"row": mate})
 
     def h_root(k):
-        return rdma(hsum.at[k], hslot.at[k, y], hs.at[k, 1], hr.at[k, 3 + y], {"row": root})
+        return rdma(hsum.at[k], hslot.at[k, y], hs.at[2 + k], hq.at[k, y], {"row": root})
 
     def h_twin(k):
-        return rdma(hsum.at[k], htwin.at[k], hs.at[k, 2], hr.at[k, 1], {"col": twin})
-
-    def h_full(k):
-        return rdma(hfull.at[k, c], hfull.at[k, c], hs.at[k, 3], hr.at[k, 2], {"row": mate})
+        return rdma(hsum.at[k], htwin.at[k], hs.at[2 + k], hr.at[2 + k], {"col": twin})
+
+    def h_full():
+        return rdma(hfull.at[c], hfull.at[c], hs.at[4], hr.at[4], {"row": mate})
 
     def d_copy(k, src, i, dev):
         return rdma(src, gd.at[k], ds.at[i], dr.at[k], dev)
@@ -228,13 +255,21 @@
         d_copy(k, gd.at[k], 0, {"row": mate}).wait_recv()
 
     def s_down(k):
-        return rdma(sbuf.at[p, k], sbuf.at[p, k], ss.at[k, 0], sr.at[p, k], {"col": lower})
+        return rdma(sbuf.at[p, k], sbuf.at[p, k], ss.at[0], sm.at[k], {"col": lower})
 
     def s_cross(k):
-        return rdma(sbuf.at[p, k], sbuf.at[p, k], ss.at[k, 1], sr.at[p, k], {"col": twin})
-
-    def s_wait(s, k):
-        rdma(sbuf.at[s, k], sbuf.at[s, k], ss.at[k, 0], sr.at[s, k], {"col": twin}).wait_recv()
+        return rdma(sbuf.at[p, k], sbuf.at[p, k], ss.at[1], sx.at[0], {"col": twin})
+
+    def s_main(k):
+        s_down(k).wait_recv()
+
+    def s_twin():
+        ref = sbuf.at[1 - p]
+        rdma(ref, ref, ss.at[1], sx.at[0], {"col": twin}).wait_recv()
+
+    def s_sent(k):
+        ref = sbuf.at[p]
+        rdma(ref, ref, ss.at[k], sx.at[0], {"col": twin}).wait_send()
 
     @pl.when(top)
     def _():
@@ -294,10 +329,12 @@
 
     @pl.when(jnp.logical_not(panel))
     def _():
+        loaded(1, 2, 3, 4)
+
         def relay(t, work=()):
             for k in range(SUB):
                 with jax.named_scope("w_main"):
-                    g_wait(p, t, k)
+                    g_main(t, k)
 
                 @pl.when(below)
                 def _():
@@ -309,8 +346,7 @@
 
         def use(t):
             with jax.named_scope("w_cross"):
-                for k in range(SUB):
-                    g_wait(1 - p, t, k)
+                g_twin(t)
             right = mat(lv, first + t)
             add_h(0, mat(gbuf, 0, t), right)
             add_h(1, mat(gbuf, 1, t), right)
@@ -334,7 +370,7 @@
             @pl.when(main_l)
             def _():
                 def step(k):
-                    l_wait(p, c, k)
+                    l_main(k)
 
                     @pl.when(below)
                     def _():
@@ -352,16 +388,16 @@
             @pl.when(other_l)
             def _():
                 def step(k):
-                    l_wait(1 - p, c, k)
+                    l_twin(k)
                     l_mate(1 - p, k).start()
 
                 loop(0, SUB, step)
 
-            loop(0, SUB, lambda k: l_wait(0, 1 - c, k))
+            l_full(0)
 
             @pl.when(c == 0)
             def _():
-                loop(0, SUB, lambda k: l_wait(1, 1, k))
+                l_full(1)
 
         start_inverse(0)
         start_inverse(1)
@@ -440,7 +476,7 @@
         def _():
             def s_relay(k):
                 with jax.named_scope("w_s"):
-                    s_wait(p, k)
+                    s_main(k)
 
                 @pl.when(below)
                 def _():
@@ -453,7 +489,7 @@
             loop(lows, n, low)
             loop(0, loc, upper)
             with jax.named_scope("w_s2"):
-                loop(0, CHUNKS, lambda k: s_wait(1 - p, k))
+                s_twin()
             k0, k1 = mat(lk, 0).astype(F32), mat(lk, 1).astype(F32)
             total = mat(gv, loc).astype(F32) - dot3(mat(sbuf, 0), k0) - dot3(mat(sbuf, 1), k1)
             with jax.named_scope("w_tmate2"):
@@ -469,32 +505,24 @@
         drain = jax.named_scope("drain")
         drain.__enter__()
 
-        def drain_g(t):
-            for k in range(SUB):
-
-                @pl.when(below)
-                def _():
-                    g_down(t, k, gbuf.at[p, t]).wait_send()
-
-                g_cross(t, k, gbuf.at[p, t]).wait_send()
-
-        loop(0, n, drain_g)
+        g_sent(1, gbuf.at[p])
+
+        @pl.when(below)
+        def _():
+            g_sent(0, gbuf.at[p])
 
         @pl.when(main_l)
         def _():
-            def step(k):
-                @pl.when(below)
-                def _():
-                    l_down(k, lbuf.at[p, c]).wait_send()
-
-                l_cross(k, lbuf.at[p, c]).wait_send()
-                l_mate(p, k).wait_send()
-
-            loop(0, SUB, step)
+            l_sent(1)
+            l_sent(2 + p)
+
+            @pl.when(below)
+            def _():
+                l_sent(0)
 
         @pl.when(other_l)
         def _():
-            loop(0, SUB, lambda k: l_mate(1 - p, k).wait_send())
+            l_sent(3 - p)
 
         t_mate().wait_send()
 
@@ -504,14 +532,11 @@
 
         @pl.when(top)
         def _():
-            def drain_s(k):
-                @pl.when(below)
-                def _():
-                    s_down(k).wait_send()
-
-                s_cross(k).wait_send()
-
-            loop(0, CHUNKS, drain_s)
+            s_sent(1)
+
+            @pl.when(below)
+            def _():
+                s_sent(0)
 
         drain.__exit__(None, None, None)
 
@@ -529,16 +554,20 @@
         cross_hi = each(lambda t, k: g_cross(t, k, gv.at[first + t]).start())
         lead = min(2, cut)
         mid = min(cut + 2, n)
+        loaded(1)
         loop(0, head, send)
 
         @pl.when(p == 0)
         def _():
+            loaded(2)
             loop(cut, mid, cross_lo)
 
         @pl.when(p == 1)
         def _():
             loop(0, lead, cross_hi)
-
+            loaded(2)
+
+        loaded(3, 4)
         with jax.named_scope("gather"):
             gather_rows()
 
@@ -587,18 +616,18 @@
             @pl.when((p == 1) | (c == 1))
             def _():
                 def step(k):
-                    l_wait(1 - p, c, k)
+                    l_twin(k)
                     l_mate(1 - p, k).start()
 
                 loop(0, SUB, step)
 
             @pl.when(p == 1)
             def _():
-                loop(0, SUB, lambda k: l_wait(0, 1 - c, k))
+                l_full(0)
 
             @pl.when((p == 0) & (c == 0))
             def _():
-                loop(0, SUB, lambda k: l_wait(1, 1, k))
+                l_full(1)
 
         def reduce_mate(k):
             with jax.named_scope("w_hmate"):
@@ -613,9 +642,8 @@
             total = hsum[k]
             for i in range(pairs - 1):
                 with jax.named_scope("w_hroot"):
-                    rdma(
-                        hslot.at[k, i], hslot.at[k, i], hs.at[k, 1], hr.at[k, 3 + i], {"row": mate}
-                    ).wait_recv()
+                    ref = hslot.at[k, i]
+                    rdma(ref, ref, hs.at[2 + k], hq.at[k, i], {"row": mate}).wait_recv()
                 total = total + hslot[k, i]
             hsum[k] = total
             h_twin(k).start()
@@ -638,15 +666,11 @@
         loop(early + 1, n_lev + 1, level)
         finish_inverse()
 
-        def g_whole(s, t):
-            with jax.named_scope("w_x"):
-                for k in range(SUB):
-                    g_wait(s, t, k)
-
         @pl.when(p == 0)
         def _():
             def use(t):
-                g_whole(1, t)
+                with jax.named_scope("w_x"):
+                    g_twin(t)
                 add_h(1, mat(gbuf, 1, t), mat(lv, first + t))
 
             loop(0, cut, use)
@@ -654,7 +678,8 @@
         @pl.when(p == 1)
         def _():
             def use(t):
-                g_whole(0, t)
+                with jax.named_scope("w_x"):
+                    g_twin(t)
                 add_h(1, mat(gv, first + t), mat(gbuf, 0, t))
 
             loop(cut, n, use)
@@ -680,17 +705,15 @@
         def _():
             with jax.named_scope("w_htwin"):
                 for k in range(2):
-                    rdma(htwin.at[k], htwin.at[k], hs.at[k, 2], hr.at[k, 1], {"col": twin}).wait_recv()
+                    h_twin(k).wait_recv()
             mine, theirs = hsum[0], htwin[0]
-            hfull[0, c] = jnp.where(p == 0, mine, theirs)
-            hfull[2, c] = jnp.where(p == 0, theirs, mine)
-            hfull[1, c] = hsum[1] + htwin[1]
-            for k in range(3):
-                h_full(k).start()
+            hfull[c, 0] = jnp.where(p == 0, mine, theirs)
+            hfull[c, 2] = jnp.where(p == 0, theirs, mine)
+            hfull[c, 1] = hsum[1] + htwin[1]
+            h_full().start()
             with jax.named_scope("w_hfull"):
-                for k in range(3):
-                    ref = hfull.at[k, 1 - c]
-                    rdma(ref, ref, hs.at[k, 3], hr.at[k, 2], {"row": mate}).wait_recv()
+                ref = hfull.at[1 - c]
+                rdma(ref, ref, hs.at[4], hr.at[4], {"row": mate}).wait_recv()
 
                 @pl.when(c == 0)
                 def _():
@@ -706,7 +729,10 @@
             l77 = mat(lbuf, 1, 1).astype(F32)
             g_here = mat(gv, loc).astype(F32)
 
-            q77 = keep(mat(gd, 2).astype(F32) - dot3(w77, mat(hfull, 2), 0, 0))
+            def full(k):
+                return jnp.concatenate([hfull[0, k], hfull[1, k]], 0)
+
+            q77 = keep(mat(gd, 2).astype(F32) - dot3(w77, full(2), 0, 0))
             m77 = dot3(l77, q77, 0, 0)
             phi77 = keep(m77) - 0.5 * m77 * eye
 
@@ -728,12 +754,12 @@
             @pl.when(jnp.logical_not((c == 1) & (p == 1)))
             def _():
                 g76 = jnp.where(c == 1, g_here, mat(gd, 1).astype(F32))
-                q76 = g76 - dot3(w77, mat(hfull, 1), 0, 0)
+                q76 = g76 - dot3(w77, full(1), 0, 0)
                 phi76 = dot3(l77, q76, 0, 0)
 
                 @pl.when((c == 0) & (p == 0))
                 def _():
-                    t66 = dot3(w66, mat(hfull, 0), 0, 0) + dot3(w76, mat(hfull, 1), 0, 0)
+                    t66 = dot3(w66, full(0), 0, 0) + dot3(w76, full(1), 0, 0)
                     q66 = keep(g_here - t66)
                     l66, l76 = mat(lbuf, 0, 0).astype(F32), mat(lbuf, 0, 1).astype(F32)
                     m66 = dot3(l66, q66, 0, 0) + dot3(l76, q76, 0, 0)
@@ -776,7 +802,7 @@
                     store(first + t, times_x(total, 1, mat(gbuf, 1, t)))
 
                 def late(t):
-                    g_whole(1, t)
+                    g_twin(t)
                     low(t)
 
                 loop(0, cut, low)
@@ -789,18 +815,9 @@
         drain = jax.named_scope("drain")
         drain.__enter__()
 
-        def drain_l():
-            def step(k):
-                if ring > 1:
-                    l_down(k, lk.at[c]).wait_send()
-                l_cross(k, lk.at[c]).wait_send()
-
-            loop(0, SUB, step)
-
         @pl.when(p == 0)
         def _():
-            loop(cut, n, each(lambda t, k: f_cross(t, k).wait_send()))
-            drain_l()
+            g_sent(1, gbuf.at[0, pl.ds(cut, n - cut)])
 
             @pl.when(top & (c == 1))
             def _():
@@ -810,23 +827,25 @@
 
         @pl.when(p == 1)
         def _():
-            loop(0, n, each(lambda t, k: g_cross(t, k, gv.at[first + t]).wait_send()))
-
-            @pl.when(c == 1)
-            def _():
-                drain_l()
+            g_sent(1, gbuf.at[1])
 
             @pl.when(top & (c == 1))
             def _():
                 d_copy(2, gv.at[loc], 0, {"row": mate}).wait_send()
                 d_copy(2, gv.at[loc], 1, {"col": twin}).wait_send()
 
+        @pl.when((p == 0) | (c == 1))
+        def _():
+            l_sent(1)
+            if ring > 1:
+                l_sent(0)
+
         @pl.when((p == 1) | (c == 1))
         def _():
-            loop(0, SUB, lambda k: l_mate(1 - p, k).wait_send())
+            l_sent(3 - p)
 
         if ring > 1:
-            loop(0, n, each(lambda t, k: g_down(t, k, gv.at[first + t]).wait_send()))
+            g_sent(0, gbuf.at[p])
         for k in range(2):
             h_mate(k).wait_send()
 
@@ -840,10 +859,9 @@
 
         @pl.when(top)
         def _():
-            for k in range(3):
-                h_full(k).wait_send()
+            h_full().wait_send()
             if ring > 1:
-                loop(0, CHUNKS, lambda k: s_down(k).wait_send())
+                s_sent(0)
 
         drain.__exit__(None, None, None)
 
@@ -888,24 +906,29 @@
             pltpu.VMEM((2, half, tile), F32),
             pltpu.VMEM((2, pairs, half, tile), F32),
             pltpu.VMEM((2, half, tile), F32),
-            pltpu.VMEM((3, 2, half, tile), F32),
+            pltpu.VMEM((2, 3, half, tile), F32),
             pltpu.VMEM((3, *sub), BF16),
             pltpu.VMEM((2, CHUNKS, tile // CHUNKS, tile), F32),
             dma((5,)),
-            dma((n, SUB, 2)),
-            dma((2, n, SUB)),
-            dma((2, SUB, 3)),
-            dma((2, 2, SUB)),
+            dma((2,)),
+            dma((n, SUB)),
+            dma((n,)),
+            dma((4,)),
+            dma((SUB,)),
+            dma((SUB,)),
+            dma((2,)),
             dma((pairs + 1,)),
             dma((2,)),
             dma((2,)),
             dma((pairs + 1,)),
-            dma((3, 4)),
-            dma((3, 3 + pairs)),
+            dma((5,)),
+            dma((5,)),
+            dma((2, pairs)),
             dma((3,)),
             dma((3,)),
-            dma((CHUNKS, 2)),
-            dma((2, CHUNKS)),
+            dma((2,)),
+            dma((CHUNKS,)),
+            dma((1,)),
         ],
         compiler_params=pltpu.CompilerParams(
             collective_id=0, has_side_effects=True, vmem_limit_bytes=VMEM

time: 72.8 us -> 71 us (0.975)
  Pallas kernels: 70.7 us -> 68.6 us
    pallas_call x1, Pallas kernels: 70.7 us -> 68.6 us  [panel(): pl.pallas_call(functools.partial(panel_kernel, n_row, n_col), out_shape=j...]
where the time goes in v3:
time: 71 us; the launch traced here: 70.7 us
  Pallas kernels  68.6 us (97%)
  local copies, waits for them, and re-layouts  2.02 us (3%)
    pallas_call x1, Pallas kernels, panel(): pl.pallas_call(functools.partial(panel_kernel, n_row, n_col), out_shape=j...  68.6 us
    unnamed x1, local copies, waits for them, and re-layouts  2.02 us

profile of v3, /device:TPU:5, one launch (start us, length us, event | category | flops | bytes accessed | tf_op | source)
XLA Modules:
  0.0 70.7 jit_solution(11941641666864217750)
XLA Ops:
  0.0 68.6 %panel.1 = f32[16,512,128]{2,1,0:T(8,128)S(1)} custom-call(bf16[16,4,64,256]{3,2,1,0:T(8,128)(2,1)} %bitcast.4, bf16[16,4,64,256]{3,2,1,0:T(8,128)(2,1)} %bitcast.5), custom_call_target="tpu_custom_call" | custom-call | tf_op jit(solution)/shard_map/panel/pallas_call | solution.py:887
  68.7 2.0 %copy.5 = f32[16,1,256,1,256]{4,3,2,1,0:T(1,128)} copy(f32[16,1,256,1,256]{4,3,2,1,0:T(1,128)S(1)} %bitcast.3) | data formatting | bytes 8388608

commit v4 on v3

--- a/solution.py
+++ b/solution.py
@@ -60,6 +60,7 @@
     lm,
     lx,
     lf,
+    lp,
     ks,
     kr,
     ts,
@@ -90,10 +91,18 @@
     y, c = row // 2, row % 2
     panel = q == ring - 1
     top = y == pairs - 1
-    below = q > 0
-    lower = jnp.maximum(col - 2, 0)
+    hub = max(ring - 3, 0)
+    other = jnp.logical_not(panel)
+    below = (q > 0) & (q <= hub)
+    above = (q == hub) & (q < ring - 2)
+    lower = jnp.where(panel, 2 * hub + p, jnp.maximum(col - 2, 0))
+    upper_col = jnp.minimum(col + 2, n_col - 1)
+    feeder = jnp.where(q == hub, n_col - 2 + p, jnp.where(q < hub, upper_col, lower))
     twin = 2 * q + 1 - p
     mate = 2 * y + 1 - c
+    part = y % 2
+    pal = 2 * (y + 1 - 2 * part) + c
+    hs_sub = SUB // 2
     root = n_row - 2 + c
 
     rows = lax.broadcasted_iota(jnp.int32, (tile, tile), 0)
@@ -138,14 +147,19 @@
 
     greet({"col": twin})
     greet({"row": mate})
-
-    @pl.when(below)
+    greet({"row": pal})
+
+    @pl.when(below | panel)
     def _():
-        greet({"col": col - 2})
-
-    @pl.when(jnp.logical_not(panel))
+        greet({"col": lower})
+
+    @pl.when(above)
     def _():
-        greet({"col": col + 2})
+        greet({"col": upper_col})
+
+    @pl.when(other)
+    def _():
+        greet({"col": feeder})
 
     @pl.when(jnp.logical_not(top))
     def _():
@@ -161,9 +175,10 @@
         greet({"row": mate, "col": twin})
 
     heard = (
-        2
-        + below.astype(jnp.int32)
-        + jnp.logical_not(panel).astype(jnp.int32)
+        3
+        + (below | panel).astype(jnp.int32)
+        + above.astype(jnp.int32)
+        + other.astype(jnp.int32)
         + jnp.where(top, pairs - 1, 1)
         + (top & panel).astype(jnp.int32)
     )
@@ -178,6 +193,9 @@
     def g_down(t, k, src):
         return rdma(src.at[k], gbuf.at[p, t, k], gs.at[0], gm.at[t, k], {"col": lower})
 
+    def g_up(t, k, src):
+        return rdma(src.at[k], gbuf.at[p, t, k], gs.at[2], gm.at[t, k], {"col": upper_col})
+
     def g_cross(t, k, src):
         return rdma(src.at[k], gbuf.at[p, t, k], gs.at[1], gx.at[t], {"col": twin})
 
@@ -195,30 +213,42 @@
     def g_sent(k, ref):
         rdma(ref, ref, gs.at[k], gx.at[0], {"col": twin}).wait_send()
 
-    def l_down(k, src):
-        return rdma(src.at[k], lbuf.at[p, c, k], ls.at[0], lm.at[k], {"col": lower})
-
-    def l_cross(k, src):
-        return rdma(src.at[k], lbuf.at[p, c, k], ls.at[1], lx.at[k], {"col": twin})
-
-    def l_mate(s, k):
-        ref = lbuf.at[s, c, k]
-        return rdma(ref, ref, ls.at[2 + s], lf.at[s], {"row": mate})
-
-    def l_main(k):
-        ref = lbuf.at[p, c, k]
-        rdma(ref, ref, ls.at[0], lm.at[k], {"col": twin}).wait_recv()
-
-    def l_twin(k):
-        ref = lbuf.at[1 - p, c, k]
-        rdma(ref, ref, ls.at[1], lx.at[k], {"col": twin}).wait_recv()
+    def l_down(j, src):
+        k = part * hs_sub + j
+        return rdma(src.at[k], lbuf.at[p, c, k], ls.at[0], lm.at[j], {"col": lower})
+
+    def l_up(j, src):
+        k = part * hs_sub + j
+        return rdma(src.at[k], lbuf.at[p, c, k], ls.at[6], lm.at[j], {"col": upper_col})
+
+    def l_cross(j, src):
+        k = part * hs_sub + j
+        return rdma(src.at[k], lbuf.at[p, c, k], ls.at[1], lx.at[j], {"col": twin})
+
+    def l_share(s, j):
+        ref = lbuf.at[s, c, part * hs_sub + j]
+        rdma(ref, ref, ls.at[2 + s], lf.at[s], {"row": mate}).start()
+        rdma(ref, ref, ls.at[4 + s], lp.at[s], {"row": pal}).start()
+
+    def l_main(j):
+        ref = lbuf.at[p, c, part * hs_sub + j]
+        rdma(ref, ref, ls.at[0], lm.at[j], {"col": twin}).wait_recv()
+
+    def l_twin(j):
+        ref = lbuf.at[1 - p, c, part * hs_sub + j]
+        rdma(ref, ref, ls.at[1], lx.at[j], {"col": twin}).wait_recv()
+
+    def l_rest(s):
+        ref = lbuf.at[s, c, pl.ds((1 - part) * hs_sub, hs_sub)]
+        rdma(ref, ref, ls.at[4], lp.at[s], {"row": pal}).wait_recv()
+        rdma(ref, ref, ls.at[2 + s], lf.at[s], {"row": mate}).start()
 
     def l_full(s):
         ref = lbuf.at[s, 1 - c]
         rdma(ref, ref, ls.at[2], lf.at[s], {"row": mate}).wait_recv()
 
-    def l_sent(k):
-        ref = lbuf.at[0, 0]
+    def l_sent(k, whole=False):
+        ref = lbuf.at[0, 0] if whole else lbuf.at[0, 0, pl.ds(0, hs_sub)]
         rdma(ref, ref, ls.at[k], lf.at[0], {"row": mate}).wait_send()
 
     def k_star(k):
@@ -256,6 +286,9 @@
 
     def s_down(k):
         return rdma(sbuf.at[p, k], sbuf.at[p, k], ss.at[0], sm.at[k], {"col": lower})
+
+    def s_up(k):
+        return rdma(sbuf.at[p, k], sbuf.at[p, k], ss.at[2], sm.at[k], {"col": upper_col})
 
     def s_cross(k):
         return rdma(sbuf.at[p, k], sbuf.at[p, k], ss.at[1], sx.at[0], {"col": twin})
@@ -340,6 +373,10 @@
                 def _():
                     g_down(t, k, gbuf.at[p, t]).start()
 
+                @pl.when(above)
+                def _():
+                    g_up(t, k, gbuf.at[p, t]).start()
+
                 g_cross(t, k, gbuf.at[p, t]).start()
                 if k < len(work):
                     work[k]()
@@ -376,55 +413,78 @@
                     def _():
                         l_down(k, lbuf.at[p, c]).start()
 
+                    @pl.when(above)
+                    def _():
+                        l_up(k, lbuf.at[p, c]).start()
+
                     l_cross(k, lbuf.at[p, c]).start()
-                    l_mate(p, k).start()
-
-                loop(0, SUB, step)
-
-        if n > head:
-            relay(head)
-        with jax.named_scope("l_wait"):
+                    l_share(p, k)
+
+                loop(0, hs_sub, step)
+
+        def share_first():
+            @pl.when(main_l)
+            def _():
+                l_rest(p)
 
             @pl.when(other_l)
             def _():
                 def step(k):
                     l_twin(k)
-                    l_mate(1 - p, k).start()
-
-                loop(0, SUB, step)
-
+                    l_share(1 - p, k)
+
+                loop(0, hs_sub, step)
+
+        def share_rest():
+            @pl.when(other_l)
+            def _():
+                l_rest(1 - p)
+
+        def share_done():
             l_full(0)
 
             @pl.when(c == 0)
             def _():
                 l_full(1)
+
+        steps = (lambda: None, share_first, share_rest, share_done)
+        for j, share in enumerate(steps):
+            if head + j < n:
+                relay(head + j, (lambda: None, functools.partial(use, j - 1)) if j > 0 else ())
+            with jax.named_scope("l_wait"):
+                share()
+        warm = min(head + len(steps), n)
+        used = max(warm - head - 1, 0)
 
         start_inverse(0)
         start_inverse(1)
-        if n > head + 1:
-            use(0)
-
-        base = min(head + 1, n)
-        inside = min(n_lev, n - base)
+
+        base = warm
+        lag = base - used
+        double = min(n_lev // 2, n - base)
 
         def level_step(i):
-            lev = i - base + 1
+            lev = 2 * (i - base) + 1
+
+            def third():
+                inverse_level(lev + 1, 0)
+                use(i - lag)
+
             relay(
                 i,
                 (
                     lambda: inverse_level(lev, 0),
                     lambda: inverse_level(lev, 1),
-                    lambda: use(i - 2),
+                    third,
+                    lambda: inverse_level(lev + 1, 1),
                 ),
             )
 
-        loop(base, base + inside, level_step)
-
-        def level_rest(lev):
-            inverse_level(lev, 0)
-            inverse_level(lev, 1)
-
-        loop(inside + 1, n_lev + 1, level_rest)
+        loop(base, base + double, level_step)
+        used += double
+
+        def level_rest(k):
+            loop(2 * double + 1, n_lev + 1, lambda lev: inverse_level(lev, k))
 
         def x_first():
             put_x(0, dot3(w[0], mat(lk, 0).astype(F32)))
@@ -432,32 +492,51 @@
         def x_second():
             put_x(1, dot3(w[2], mat(lk, 0).astype(F32)) + dot3(w[1], mat(lk, 1).astype(F32)))
 
-        at = base + inside
+        def solve_x():
+            x_first()
+            x_second()
+            loop(used, at - 1, use)
+
+        at = base + double
         if at < n:
-            relay(at, (finish_inverse, x_first, x_second, lambda: use(at - 2)))
+            relay(at, (lambda: level_rest(0), lambda: level_rest(1), finish_inverse, solve_x))
+            used = at - 1
             at += 1
         else:
+            level_rest(0)
+            level_rest(1)
             finish_inverse()
             x_first()
             x_second()
         begun = at
 
-        per = 3 if n <= begun + 4 else 1
+        per = max(d for d in (1, 2, 3) if d == 1 or d * max(n - begun, 1) <= n - 2)
 
         def low_step(i):
             j = (i - begun) * per
-            relay(i, [functools.partial(lambda d: low(j + d), d) for d in range(per)] + [lambda: use(i - 2)])
+            relay(i, [lambda: use(i - 2)] + [functools.partial(lambda d: low(j + d), d) for d in range(per)])
 
         loop(begun, n, low_step)
         lows = per * max(n - begun, 0)
-        used = max(n - 2, 0) if n > base else 0
+        used += max(n - begun, 0)
 
         def send_t():
             loop(used, n, use)
             h0, h1 = mat(h, 0), mat(h, 1)
-            tout[1] = dot3(w[1], h1, 0, 0)
-            tout[0] = dot3(w[0], h0, 0, 0) + dot3(w[2], h1, 0, 0)
-            t_mate().start()
+
+            def first_t():
+                tout[1] = dot3(w[1], h1, 0, 0)
+
+            def second_t():
+                tout[0] = dot3(w[0], h0, 0, 0) + dot3(w[2], h1, 0, 0)
+
+            for mine, one, two in ((0, first_t, second_t), (1, second_t, first_t)):
+
+                @pl.when(c == mine)
+                def _(one=one, two=two):
+                    one()
+                    t_mate().start()
+                    two()
 
         def upper(a):
             store(a, mat(gv, a).astype(F32))
@@ -481,6 +560,10 @@
                 @pl.when(below)
                 def _():
                     s_down(k).start()
+
+                @pl.when(above)
+                def _():
+                    s_up(k).start()
 
                 s_cross(k).start()
 
@@ -511,18 +594,28 @@
         def _():
             g_sent(0, gbuf.at[p])
 
+        @pl.when(above)
+        def _():
+            g_sent(2, gbuf.at[p])
+
         @pl.when(main_l)
         def _():
             l_sent(1)
-            l_sent(2 + p)
+            l_sent(2 + p, True)
+            l_sent(4 + p)
 
             @pl.when(below)
             def _():
                 l_sent(0)
 
+            @pl.when(above)
+            def _():
+                l_sent(6)
+
         @pl.when(other_l)
         def _():
-            l_sent(3 - p)
+            l_sent(3 - p, True)
+            l_sent(5 - p)
 
         t_mate().wait_send()
 
@@ -537,6 +630,10 @@
             @pl.when(below)
             def _():
                 s_sent(0)
+
+            @pl.when(above)
+            def _():
+                s_sent(2)
 
         drain.__exit__(None, None, None)
 
@@ -577,7 +674,7 @@
                     l_down(k, lk.at[c]).start()
                 l_cross(k, lk.at[c]).start()
 
-            loop(0, SUB, step)
+            loop(0, hs_sub, step)
 
         @pl.when(p == 0)
         def _():
@@ -617,9 +714,10 @@
             def _():
                 def step(k):
                     l_twin(k)
-                    l_mate(1 - p, k).start()
-
-                loop(0, SUB, step)
+                    l_share(1 - p, k)
+
+                loop(0, hs_sub, step)
+                l_rest(1 - p)
 
             @pl.when(p == 1)
             def _():
@@ -842,7 +940,8 @@
 
         @pl.when((p == 1) | (c == 1))
         def _():
-            l_sent(3 - p)
+            l_sent(3 - p, True)
+            l_sent(5 - p)
 
         if ring > 1:
             g_sent(0, gbuf.at[p])
@@ -910,12 +1009,13 @@
             pltpu.VMEM((3, *sub), BF16),
             pltpu.VMEM((2, CHUNKS, tile // CHUNKS, tile), F32),
             dma((5,)),
-            dma((2,)),
+            dma((3,)),
             dma((n, SUB)),
             dma((n,)),
-            dma((4,)),
-            dma((SUB,)),
-            dma((SUB,)),
+            dma((7,)),
+            dma((SUB // 2,)),
+            dma((SUB // 2,)),
+            dma((2,)),
             dma((2,)),
             dma((pairs + 1,)),
             dma((2,)),
@@ -926,7 +1026,7 @@
             dma((2, pairs)),
             dma((3,)),
             dma((3,)),
-            dma((2,)),
+            dma((3,)),
             dma((CHUNKS,)),
             dma((1,)),
         ],
@@ -944,7 +1044,7 @@
     rows_here, tile = l_saved.shape[0], l_saved.shape[2]
     n_row = lax.axis_size("row")
     n_col = lax.axis_size("col")
-    assert n_col % n_row == 0 and n_row % 2 == 0 and tile % (SUB * 16) == 0
+    assert n_col % n_row == 0 and n_row % 4 == 0 and tile % (SUB * 16) == 0
     first = n_col // n_row
     factor = l_saved.reshape(rows_here, tile, tile)
     grad = l_grad.reshape(rows_here, tile, tile)

time: 71 us -> 66.6 us (0.938)
  Pallas kernels: 68.6 us -> 63.8 us
    pallas_call x1, Pallas kernels: 68.6 us -> 63.8 us  [panel(): pl.pallas_call(functools.partial(panel_kernel, n_row, n_col), out_shape=j...]
where the time goes in v4:
time: 66.6 us; the launch traced here: 65.8 us
  Pallas kernels  63.8 us (96%)
  local copies, waits for them, and re-layouts  2.02 us (3%)
    pallas_call x1, Pallas kernels, panel(): pl.pallas_call(functools.partial(panel_kernel, n_row, n_col), out_shape=j...  63.8 us
    unnamed x1, local copies, waits for them, and re-layouts  2.02 us

profile of v4, /device:TPU:5, one launch (start us, length us, event | category | flops | bytes accessed | tf_op | source)
XLA Modules:
  0.0 65.8 jit_solution(8322373620969495625)
XLA Ops:
  0.0 63.8 %panel.1 = f32[16,512,128]{2,1,0:T(8,128)S(1)} custom-call(bf16[16,4,64,256]{3,2,1,0:T(8,128)(2,1)} %bitcast.4, bf16[16,4,64,256]{3,2,1,0:T(8,128)(2,1)} %bitcast.5), custom_call_target="tpu_custom_call" | custom-call | tf_op jit(solution)/shard_map/panel/pallas_call | solution.py:986
  63.8 2.0 %copy.5 = f32[16,1,256,1,256]{4,3,2,1,0:T(1,128)} copy(f32[16,1,256,1,256]{4,3,2,1,0:T(1,128)S(1)} %bitcast.3) | data formatting | bytes 8388608

commit v5 on v4

--- a/solution.py
+++ b/solution.py
@@ -100,9 +100,8 @@
     feeder = jnp.where(q == hub, n_col - 2 + p, jnp.where(q < hub, upper_col, lower))
     twin = 2 * q + 1 - p
     mate = 2 * y + 1 - c
-    part = y % 2
-    pal = 2 * (y + 1 - 2 * part) + c
-    hs_sub = SUB // 2
+    odd = y % 2 == 1
+    pal = 2 * (y + 1 - 2 * (y % 2)) + c
     root = n_row - 2 + c
 
     rows = lax.broadcasted_iota(jnp.int32, (tile, tile), 0)
@@ -213,33 +212,30 @@
     def g_sent(k, ref):
         rdma(ref, ref, gs.at[k], gx.at[0], {"col": twin}).wait_send()
 
-    def l_down(j, src):
-        k = part * hs_sub + j
-        return rdma(src.at[k], lbuf.at[p, c, k], ls.at[0], lm.at[j], {"col": lower})
-
-    def l_up(j, src):
-        k = part * hs_sub + j
-        return rdma(src.at[k], lbuf.at[p, c, k], ls.at[6], lm.at[j], {"col": upper_col})
-
-    def l_cross(j, src):
-        k = part * hs_sub + j
-        return rdma(src.at[k], lbuf.at[p, c, k], ls.at[1], lx.at[j], {"col": twin})
-
-    def l_share(s, j):
-        ref = lbuf.at[s, c, part * hs_sub + j]
+    def l_down(k, src):
+        return rdma(src.at[k], lbuf.at[p, c, k], ls.at[0], lm.at[k], {"col": lower})
+
+    def l_up(k, src):
+        return rdma(src.at[k], lbuf.at[p, c, k], ls.at[6], lm.at[k], {"col": upper_col})
+
+    def l_cross(k, src):
+        return rdma(src.at[k], lbuf.at[p, c, k], ls.at[1], lx.at[k], {"col": twin})
+
+    def l_share(s, k):
+        ref = lbuf.at[s, c, k]
+        rdma(ref, ref, ls.at[4 + s], lp.at[s], {"row": pal}).start()
         rdma(ref, ref, ls.at[2 + s], lf.at[s], {"row": mate}).start()
-        rdma(ref, ref, ls.at[4 + s], lp.at[s], {"row": pal}).start()
-
-    def l_main(j):
-        ref = lbuf.at[p, c, part * hs_sub + j]
-        rdma(ref, ref, ls.at[0], lm.at[j], {"col": twin}).wait_recv()
-
-    def l_twin(j):
-        ref = lbuf.at[1 - p, c, part * hs_sub + j]
-        rdma(ref, ref, ls.at[1], lx.at[j], {"col": twin}).wait_recv()
+
+    def l_main(k):
+        ref = lbuf.at[p, c, k]
+        rdma(ref, ref, ls.at[0], lm.at[k], {"col": twin}).wait_recv()
+
+    def l_twin(k):
+        ref = lbuf.at[1 - p, c, k]
+        rdma(ref, ref, ls.at[1], lx.at[k], {"col": twin}).wait_recv()
 
     def l_rest(s):
-        ref = lbuf.at[s, c, pl.ds((1 - part) * hs_sub, hs_sub)]
+        ref = lbuf.at[s, c]
         rdma(ref, ref, ls.at[4], lp.at[s], {"row": pal}).wait_recv()
         rdma(ref, ref, ls.at[2 + s], lf.at[s], {"row": mate}).start()
 
@@ -247,8 +243,8 @@
         ref = lbuf.at[s, 1 - c]
         rdma(ref, ref, ls.at[2], lf.at[s], {"row": mate}).wait_recv()
 
-    def l_sent(k, whole=False):
-        ref = lbuf.at[0, 0] if whole else lbuf.at[0, 0, pl.ds(0, hs_sub)]
+    def l_sent(k):
+        ref = lbuf.at[0, 0]
         rdma(ref, ref, ls.at[k], lf.at[0], {"row": mate}).wait_send()
 
     def k_star(k):
@@ -316,8 +312,6 @@
         def _():
             k_wait(c)
             k_mate(lk.at[c]).start()
-
-        k_wait(1 - c)
 
     def start_inverse(k):
         d = mat(lbuf, k, k).astype(F32)
@@ -399,12 +393,13 @@
 
         for t in range(head):
             relay(t)
-        with jax.named_scope("gather"):
-            gather_rows()
+            if t == 0:
+                with jax.named_scope("gather"):
+                    gather_rows()
 
         with jax.named_scope("l_relay"):
 
-            @pl.when(main_l)
+            @pl.when(main_l & odd)
             def _():
                 def step(k):
                     l_main(k)
@@ -420,34 +415,35 @@
                     l_cross(k, lbuf.at[p, c]).start()
                     l_share(p, k)
 
-                loop(0, hs_sub, step)
+                loop(0, SUB, step)
 
         def share_first():
-            @pl.when(main_l)
+            @pl.when(main_l & jnp.logical_not(odd))
             def _():
                 l_rest(p)
 
-            @pl.when(other_l)
+            @pl.when(other_l & odd)
             def _():
                 def step(k):
                     l_twin(k)
                     l_share(1 - p, k)
 
-                loop(0, hs_sub, step)
+                loop(0, SUB, step)
 
         def share_rest():
-            @pl.when(other_l)
+            @pl.when(other_l & jnp.logical_not(odd))
             def _():
                 l_rest(1 - p)
 
         def share_done():
+            k_wait(1 - c)
             l_full(0)
 
             @pl.when(c == 0)
             def _():
                 l_full(1)
 
-        steps = (lambda: None, share_first, share_rest, share_done)
+        steps = (lambda: None, share_first, lambda: None, share_rest, share_done)
         for j, share in enumerate(steps):
             if head + j < n:
                 relay(head + j, (lambda: None, functools.partial(use, j - 1)) if j > 0 else ())
@@ -600,22 +596,28 @@
 
         @pl.when(main_l)
         def _():
-            l_sent(1)
-            l_sent(2 + p, True)
-            l_sent(4 + p)
-
-            @pl.when(below)
+            l_sent(2 + p)
+
+            @pl.when(odd)
+            def _():
+                l_sent(1)
+                l_sent(4 + p)
+
+            @pl.when(odd & below)
             def _():
                 l_sent(0)
 
-            @pl.when(above)
+            @pl.when(odd & above)
             def _():
                 l_sent(6)
 
         @pl.when(other_l)
         def _():
-            l_sent(3 - p, True)
-            l_sent(5 - p)
+            l_sent(3 - p)
+
+            @pl.when(odd)
+            def _():
+                l_sent(5 - p)
 
         t_mate().wait_send()
 
@@ -665,16 +667,23 @@
             loaded(2)
 
         loaded(3, 4)
+        @pl.when(jnp.logical_not(odd))
+        def _():
+            loop(head, n, send)
+
         with jax.named_scope("gather"):
             gather_rows()
+            k_wait(1 - c)
 
         def send_l():
-            def step(k):
-                if ring > 1:
-                    l_down(k, lk.at[c]).start()
-                l_cross(k, lk.at[c]).start()
-
-            loop(0, hs_sub, step)
+            @pl.when(odd)
+            def _():
+                def step(k):
+                    if ring > 1:
+                        l_down(k, lk.at[c]).start()
+                    l_cross(k, lk.at[c]).start()
+
+                loop(0, SUB, step)
 
         @pl.when(p == 0)
         def _():
@@ -703,20 +712,25 @@
                 d_copy(2, gv.at[loc], 1, {"col": twin}).start()
                 gd[2] = gv[loc]
 
-        loop(head, n, send)
+        @pl.when(odd)
+        def _():
+            loop(head, n, send)
 
         with jax.named_scope("hd"):
             loop(0, n, lambda t: add_h(0, mat(gv, first + t), mat(lv, first + t)))
         h_mate(0).start()
 
         with jax.named_scope("l_wait"):
-            @pl.when((p == 1) | (c == 1))
+            @pl.when(((p == 1) | (c == 1)) & odd)
             def _():
                 def step(k):
                     l_twin(k)
                     l_share(1 - p, k)
 
-                loop(0, hs_sub, step)
+                loop(0, SUB, step)
+
+            @pl.when(((p == 1) | (c == 1)) & jnp.logical_not(odd))
+            def _():
                 l_rest(1 - p)
 
             @pl.when(p == 1)
@@ -932,7 +946,7 @@
                 d_copy(2, gv.at[loc], 0, {"row": mate}).wait_send()
                 d_copy(2, gv.at[loc], 1, {"col": twin}).wait_send()
 
-        @pl.when((p == 0) | (c == 1))
+        @pl.when(((p == 0) | (c == 1)) & odd)
         def _():
             l_sent(1)
             if ring > 1:
@@ -940,8 +954,11 @@
 
         @pl.when((p == 1) | (c == 1))
         def _():
-            l_sent(3 - p, True)
-            l_sent(5 - p)
+            l_sent(3 - p)
+
+            @pl.when(odd)
+            def _():
+                l_sent(5 - p)
 
         if ring > 1:
             g_sent(0, gbuf.at[p])
@@ -1013,8 +1030,8 @@
             dma((n, SUB)),
             dma((n,)),
             dma((7,)),
-            dma((SUB // 2,)),
-            dma((SUB // 2,)),
+            dma((SUB,)),
+            dma((SUB,)),
             dma((2,)),
             dma((2,)),
             dma((pairs + 1,)),

time: 66.6 us -> 64.8 us (0.973)
  Pallas kernels: 63.8 us -> 62.6 us
    pallas_call x1, Pallas kernels: 63.8 us -> 62.6 us  [panel(): pl.pallas_call(functools.partial(panel_kernel, n_row, n_col), out_shape=j...]
where the time goes in v5:
time: 64.8 us; the launch traced here: 64.6 us
  Pallas kernels  62.6 us (97%)
  local copies, waits for them, and re-layouts  2.02 us (3%)
    pallas_call x1, Pallas kernels, panel(): pl.pallas_call(functools.partial(panel_kernel, n_row, n_col), out_shape=j...  62.6 us
    unnamed x1, local copies, waits for them, and re-layouts  2.02 us

profile of v5, /device:TPU:5, one launch (start us, length us, event | category | flops | bytes accessed | tf_op | source)
XLA Modules:
  0.0 64.6 jit_solution(13549187872690826237)
XLA Ops:
  0.0 62.6 %panel.1 = f32[16,512,128]{2,1,0:T(8,128)S(1)} custom-call(bf16[16,4,64,256]{3,2,1,0:T(8,128)(2,1)} %bitcast.4, bf16[16,4,64,256]{3,2,1,0:T(8,128)(2,1)} %bitcast.5), custom_call_target="tpu_custom_call" | custom-call | tf_op jit(solution)/shard_map/panel/pallas_call | solution.py:1003
  62.6 2.0 %copy.5 = f32[16,1,256,1,256]{4,3,2,1,0:T(1,128)} copy(f32[16,1,256,1,256]{4,3,2,1,0:T(1,128)S(1)} %bitcast.3) | data formatting | bytes 8388608

commit v6 on v5

--- a/solution.py
+++ b/solution.py
@@ -42,6 +42,7 @@
     lbuf,
     w,
     h,
+    own,
     tout,
     tin,
     tslot,
@@ -257,10 +258,13 @@
         rdma(lk.at[i], lk.at[i], ks.at[pairs], kr.at[i], {"row": mate}).wait_recv()
 
     def t_mate():
-        return rdma(tout.at[1 - c], tin, ts.at[0], tr.at[pairs], {"row": mate})
+        return rdma(h.at[1 - c], tin, ts.at[0], tr.at[pairs], {"row": mate})
 
     def t_root():
-        return rdma(tout.at[c], tslot.at[y], ts.at[1], tr.at[y], {"row": root})
+        return rdma(tout.at[0], tslot.at[y], ts.at[1], tr.at[y], {"row": root})
+
+    def t_all():
+        return rdma(tout.at[0], tout.at[1], ts.at[2], tr.at[pairs + 1], {"row": mate})
 
     def h_mate(k):
         return rdma(h.at[k, 1 - c], hin.at[k], hs.at[k], hr.at[k], {"row": mate})
@@ -516,34 +520,49 @@
         lows = per * max(n - begun, 0)
         used += max(n - begun, 0)
 
-        def send_t():
-            loop(used, n, use)
-            h0, h1 = mat(h, 0), mat(h, 1)
-
-            def first_t():
-                tout[1] = dot3(w[1], h1, 0, 0)
-
-            def second_t():
-                tout[0] = dot3(w[0], h0, 0, 0) + dot3(w[2], h1, 0, 0)
-
-            for mine, one, two in ((0, first_t, second_t), (1, second_t, first_t)):
-
-                @pl.when(c == mine)
-                def _(one=one, two=two):
-                    one()
-                    t_mate().start()
-                    two()
+        def use_main(t):
+            add_h(p, mat(gbuf, p, t), mat(lv, first + t))
+
+        def use_twin(t):
+            with jax.named_scope("w_cross"):
+                g_twin(t)
+            add_h(1 - p, mat(gbuf, 1 - p, t), mat(lv, first + t))
+
+        def give():
+            t_mate().start()
+
+        def take():
+            with jax.named_scope("w_tmate"):
+                t_mate().wait_recv()
+            tout[0] = h[c] + tin[...]
 
         def upper(a):
             store(a, mat(gv, a).astype(F32))
 
         @pl.when(jnp.logical_not(top))
         def _():
-            send_t()
-            with jax.named_scope("w_tmate"):
-                t_mate().wait_recv()
-            tout[c] += tin[...]
-            t_root().start()
+            loop(used, n, use_main)
+
+            @pl.when(c != p)
+            def _():
+                give()
+
+            @pl.when(c == p)
+            def _():
+                take()
+                t_root().start()
+
+            loop(used, n, use_twin)
+
+            @pl.when(c == p)
+            def _():
+                give()
+
+            @pl.when(c != p)
+            def _():
+                take()
+                t_root().start()
+
             loop(lows, n, low)
             loop(0, loc + 1, upper)
 
@@ -563,23 +582,58 @@
 
                 s_cross(k).start()
 
-            loop(0, CHUNKS, s_relay)
-            send_t()
-            loop(lows, n, low)
+            early = max(min(CHUNKS, used - lows), 0)
+
+            def give_twin():
+                @pl.when(c == p)
+                def _():
+                    give()
+
+            loop(used, n, use_main)
+
+            @pl.when(c != p)
+            def _():
+                give()
+
+            rest = list(range(used, n))
+            for k in range(CHUNKS):
+                s_relay(k)
+                if k < early:
+                    low(lows + k)
+                if rest and k % 2 == 1 and k >= CHUNKS // 2 - 1:
+                    use_twin(rest.pop(0))
+                    if not rest:
+                        give_twin()
+            if rest:
+                loop(rest[0], n, use_twin)
+                give_twin()
+
+            loop(lows + early, n, low)
             loop(0, loc, upper)
-            with jax.named_scope("w_s2"):
-                s_twin()
-            k0, k1 = mat(lk, 0).astype(F32), mat(lk, 1).astype(F32)
-            total = mat(gv, loc).astype(F32) - dot3(mat(sbuf, 0), k0) - dot3(mat(sbuf, 1), k1)
-            with jax.named_scope("w_tmate2"):
-                t_mate().wait_recv()
-            total = total - (tout[c] + tin[...])
+            total = mat(gv, loc).astype(F32) - dot3(mat(sbuf, p), mat(lk, p).astype(F32))
+            take()
             with jax.named_scope("w_tslot"):
                 for k in range(pairs - 1):
                     rdma(tslot.at[k], tslot.at[k], ts.at[1], tr.at[k], {"row": mate}).wait_recv()
             for k in range(pairs - 1):
-                total = total - tslot[k]
-            store(loc, total)
+                tout[0] += tslot[k]
+            own[...] = total
+
+            @pl.when(c == 1)
+            def _():
+                t_all().start()
+                own[...] -= dot3(w[1], mat(tout, 0), 0, 0)
+
+            @pl.when(c == 0)
+            def _():
+                own[...] -= dot3(w[0], mat(tout, 0), 0, 0)
+                with jax.named_scope("w_tall"):
+                    t_all().wait_recv()
+                own[...] -= dot3(w[2], mat(tout, 1), 0, 0)
+
+            with jax.named_scope("w_s2"):
+                s_twin()
+            store(loc, own[...] - dot3(mat(sbuf, 1 - p), mat(lk, 1 - p).astype(F32)))
 
         drain = jax.named_scope("drain")
         drain.__enter__()
@@ -624,6 +678,10 @@
         @pl.when(jnp.logical_not(top))
         def _():
             t_root().wait_send()
+
+        @pl.when(top & (c == 1))
+        def _():
+            t_all().wait_send()
 
         @pl.when(top)
         def _():
@@ -1015,9 +1073,10 @@
             pltpu.VMEM((2, 2, *sub), BF16),
             pltpu.VMEM((3, tile, tile), F32),
             pltpu.VMEM((2, 2, half, tile), F32),
-            pltpu.VMEM((2, tile, tile), F32),
             pltpu.VMEM((tile, tile), F32),
-            pltpu.VMEM((pairs, tile, tile), F32),
+            pltpu.VMEM((2, 2, half, tile), F32),
+            pltpu.VMEM((2, half, tile), F32),
+            pltpu.VMEM((pairs, 2, half, tile), F32),
             pltpu.VMEM((2, half, tile), F32),
             pltpu.VMEM((2, half, tile), F32),
             pltpu.VMEM((2, pairs, half, tile), F32),
@@ -1036,8 +1095,8 @@
             dma((2,)),
             dma((pairs + 1,)),
             dma((2,)),
-            dma((2,)),
-            dma((pairs + 1,)),
+            dma((3,)),
+            dma((pairs + 2,)),
             dma((5,)),
             dma((5,)),
             dma((2, pairs)),

time: 64.8 us -> 63.7 us (0.983)
  Pallas kernels: 62.6 us -> 60.9 us
    pallas_call x1, Pallas kernels: 62.6 us -> 60.9 us  [panel(): pl.pallas_call(functools.partial(panel_kernel, n_row, n_col), out_shape=j...]
where the time goes in v6:
time: 63.7 us; the launch traced here: 63 us
  Pallas kernels  60.9 us (96%)
  local copies, waits for them, and re-layouts  2.02 us (3%)
    pallas_call x1, Pallas kernels, panel(): pl.pallas_call(functools.partial(panel_kernel, n_row, n_col), out_shape=j...  60.9 us
    unnamed x1, local copies, waits for them, and re-layouts  2.02 us

profile of v6, /device:TPU:5, one launch (start us, length us, event | category | flops | bytes accessed | tf_op | source)
XLA Modules:
  0.0 63.0 jit_solution(13282259783855399686)
XLA Ops:
  0.0 60.9 %panel.1 = f32[16,512,128]{2,1,0:T(8,128)S(1)} custom-call(bf16[16,4,64,256]{3,2,1,0:T(8,128)(2,1)} %bitcast.4, bf16[16,4,64,256]{3,2,1,0:T(8,128)(2,1)} %bitcast.5), custom_call_target="tpu_custom_call" | custom-call | tf_op jit(solution)/shard_map/panel/pallas_call | solution.py:1061
  61.0 2.0 %copy.5 = f32[16,1,256,1,256]{4,3,2,1,0:T(1,128)} copy(f32[16,1,256,1,256]{4,3,2,1,0:T(1,128)S(1)} %bitcast.3) | data formatting | bytes 8388608

commit v7 on v6

--- a/solution.py
+++ b/solution.py
@@ -82,7 +82,7 @@
     loc = first - 1
     ring = n_col // 2
     cut = n // 2
-    head = min(2, n)
+    head = min(1, n)
     pairs = n_row // 2
     parts = tile // LANE
 
@@ -447,7 +447,7 @@
             def _():
                 l_full(1)
 
-        steps = (lambda: None, share_first, lambda: None, share_rest, share_done)
+        steps = (lambda: None, lambda: None, share_first, lambda: None, share_rest, share_done)
         for j, share in enumerate(steps):
             if head + j < n:
                 relay(head + j, (lambda: None, functools.partial(use, j - 1)) if j > 0 else ())
@@ -709,7 +709,7 @@
         send = each(lambda t, k: g_down(t, k, gv.at[first + t]).start() if ring > 1 else None)
         cross_lo = each(lambda t, k: f_cross(t, k).start())
         cross_hi = each(lambda t, k: g_cross(t, k, gv.at[first + t]).start())
-        lead = min(2, cut)
+        lead = min(head, cut)
         mid = min(cut + 2, n)
         loaded(1)
         loop(0, head, send)

time: 63.7 us -> 63.8 us (level)
  no operation moved by 1% of the time
where the time goes in v7:
time: 63.8 us; the launch traced here: 63.1 us
  Pallas kernels  61 us (96%)
  local copies, waits for them, and re-layouts  2.02 us (3%)
    pallas_call x1, Pallas kernels, panel(): pl.pallas_call(functools.partial(panel_kernel, n_row, n_col), out_shape=j...  61 us
    unnamed x1, local copies, waits for them, and re-layouts  2.02 us

profile of v7, /device:TPU:5, one launch (start us, length us, event | category | flops | bytes accessed | tf_op | source)
XLA Modules:
  0.0 63.1 jit_solution(4520172637569218580)
XLA Ops:
  0.0 61.0 %panel.1 = f32[16,512,128]{2,1,0:T(8,128)S(1)} custom-call(bf16[16,4,64,256]{3,2,1,0:T(8,128)(2,1)} %bitcast.4, bf16[16,4,64,256]{3,2,1,0:T(8,128)(2,1)} %bitcast.5), custom_call_target="tpu_custom_call" | custom-call | tf_op jit(solution)/shard_map/panel/pallas_call | solution.py:1061
  61.0 2.0 %copy.5 = f32[16,1,256,1,256]{4,3,2,1,0:T(1,128)} copy(f32[16,1,256,1,256]{4,3,2,1,0:T(1,128)S(1)} %bitcast.3) | data formatting | bytes 8388608
